TPU v7x, 32 devices: a whole 2x2x4 slice. The times are simulated.
32 devices in a mesh: row: 4 (over z), col: 2 (over x), depth: 4 (over y, core).
Axes of the slice: x: 2, y: 2, z: 4, core: 2. Of those that a mesh axis runs over, the one named last changes fastest.
Arguments:
- pair_input: bfloat16 [192, 192, 128], P('row', ('col', 'depth')), may hold values from -40 to 40
- in_gain: float32 [128], replicated, may hold values from 0.1 to 1.9
- in_shift: float32 [128], replicated, may hold values from -3 to 3
- w_proj: bfloat16 [128, 512], replicated, may hold values from -0.5 to 0.5
- w_gate: bfloat16 [128, 128], replicated, may hold values from -0.5 to 0.5
- out_gain: float32 [128], replicated, may hold values from 0.1 to 1.9
- out_shift: float32 [128], replicated, may hold values from -3 to 3
- w_out: bfloat16 [128, 128], replicated, may hold values from -0.5 to 0.5
Outputs:
- update: bfloat16 [192, 192, 128], P('row', ('col', 'depth'))
All inputs are finite; a program needn't handle non-finite values.
Results may differ from a plain program's by a relative error of at most 0.013.
Values may be sent and summed in bfloat16 or wider, within the bound.
No kernel may reach another device: no remote copies, remote signals or barrier semaphores. Data moves between devices by JAX's collectives and lax.ppermute only.
A program may use at most 64 MiB of HBM per device.

v0:
```python
import jax
import jax.numpy as jnp
from jax import lax
from jax.sharding import PartitionSpec as P


def layer_norm(values, scaling, offsets):
    average = jnp.mean(values, axis=-1, keepdims=True)
    centred = values - average
    variance = jnp.mean(centred * centred, axis=-1, keepdims=True)
    return centred * lax.rsqrt(variance + 1e-05) * scaling + offsets


def gated_sides(normed, w_proj):
    channels = w_proj.shape[1] // 4
    projected = jnp.einsum("xyc,cd->xyd", normed, w_proj, preferred_element_type=jnp.float32)
    left_side = (
        jax.nn.sigmoid(projected[..., :channels]) * projected[..., channels : 2 * channels]
    ).astype(jnp.bfloat16)
    right_side = (
        jax.nn.sigmoid(projected[..., 2 * channels : 3 * channels]) * projected[..., 3 * channels :]
    ).astype(jnp.bfloat16)
    return (left_side, right_side)


def reorder_channels(values, row_count, other_count):
    shape_rest = values.shape[1:]
    grouped = values.reshape((row_count, other_count, -1) + shape_rest)
    return jnp.swapaxes(grouped, 0, 1).reshape(values.shape)


def per_device(pair_input, in_gain, in_shift, w_proj, w_gate, out_gain, out_shift, w_out):
    row_count = lax.axis_size("row")
    col_count = lax.axis_size("col")
    depth_count = lax.axis_size("depth")
    normed = layer_norm(pair_input.astype(jnp.float32), in_gain, in_shift).astype(jnp.bfloat16)
    left_side, right_side = gated_sides(normed, w_proj)
    left_all, right_all = (
        lax.all_to_all(
            lax.all_to_all(left_side, "row", split_axis=2, concat_axis=0, tiled=True),
            ("col", "depth"),
            split_axis=2,
            concat_axis=1,
            tiled=True,
        ),
        lax.all_to_all(
            lax.all_to_all(right_side, "row", split_axis=2, concat_axis=0, tiled=True),
            ("col", "depth"),
            split_axis=2,
            concat_axis=1,
            tiled=True,
        ),
    )
    planes = jnp.einsum("kic,kjc->ijc", left_all, right_all, preferred_element_type=jnp.float32)
    product = lax.all_to_all(
        lax.all_to_all(planes.astype(jnp.bfloat16), "row", split_axis=0, concat_axis=2, tiled=True),
        ("col", "depth"),
        split_axis=1,
        concat_axis=2,
        tiled=True,
    ).astype(planes.dtype)
    other_count = col_count * depth_count
    used_gain = reorder_channels(out_gain, row_count, other_count)
    used_shift = reorder_channels(out_shift, row_count, other_count)
    used_out = reorder_channels(w_out, row_count, other_count)
    product_norm = layer_norm(product, used_gain, used_shift).astype(jnp.bfloat16)
    gating = jax.nn.sigmoid(
        jnp.einsum("xyc,cd->xyd", normed, w_gate, preferred_element_type=jnp.float32)
    )
    projected_out = jnp.einsum(
        "xyc,cd->xyd", product_norm, used_out, preferred_element_type=jnp.float32
    )
    return (gating * projected_out).astype(jnp.bfloat16)


def solution(mesh):
    placed = (P("row", ("col", "depth"), None), P(), P(), P(), P(), P(), P(), P())
    return jax.shard_map(
        per_device,
        mesh=mesh,
        in_specs=placed,
        out_specs=P("row", ("col", "depth"), None),
        check_vma=False,
    )
```

profile of v0, /device:TPU:0, one launch (start us, length us, event | category | flops | bytes accessed | tf_op | source)
XLA Modules:
  0.0 87.3 jit_solution(1574282504677348500)
XLA Ops:
  0.0 1.2 %convert_reduce_fusion = f32[48,24]{1,0:T(8,128)S(1)} fusion(bf16[48,24,128]{2,1,0:T(8,128)(2,1)} %param.8), kind=kLoop, calls=%fused_computation.18 | loop fusion | flops 293760 | bytes 299520 | tf_op jit(solution)/shard_map/reduce_sum | solution.py:8
  1.2 0.1 copy.85
  1.3 0.1 copy.86
  1.4 1.4 %fusion.15 = f32[48,24]{1,0:T(8,128)S(1)} fusion(bf16[48,24,128]{2,1,0:T(8,128)(2,1)} %param.8, f32[48,24]{1,0:T(8,128)S(1)} %copy.86), kind=kLoop, calls=%fused_computation.21 | loop fusion | flops 588672 | bytes 304128 | tf_op jit(solution)/shard_map/reduce_sum | solution.py:10
  2.8 0.1 copy.87
  2.8 0.1 copy.88
  2.9 1.6 %fusion.27 = f32[48,24,512]{2,1,0:T(8,128)S(1)} fusion(bf16[128,512]{1,0:T(8,128)(2,1)S(1)} %copy-done, bf16[48,24,128]{2,1,0:T(8,128)(2,1)} %param.8, f32[128]{0:T(128)} %param.10, f32[128]{0:T(128)} %param.9, f32[48,24]{1,0:T(8,128)S(1)} %copy.88, f32[48,24]{1,0:T(8,128)S(1)} %copy.86), kind=kOutput, calls=%fused_computation.37 | convolution fusion | flops 151879680 | bytes 2795520 | tf_op jit(solution)/shard_map/xyc,cd->xyd/dot_general | solution.py:16
  4.5 0.3 fusion.19
  4.8 0.5 copy.94
  5.3 2.0 %reshape.59 = bf16[4,2,18432]{2,1,0:T(2,128)(2,1)} reshape(bf16[128,24,48]{2,1,0:T(8,128)(2,1)S(1)} %bitcast.78) | data formatting | bytes 589824
  7.3 6.3 %all-to-all-start.2 = ((bf16[4,2,18432]{2,1,0:T(2,128)(2,1)}), bf16[4,2,18432]{2,1,0:T(2,128)(2,1)S(1)}, u32[]{:S(2)}, u32[]{:S(2)}) async-start(bf16[4,2,18432]{2,1,0:T(2,128)(2,1)} %reshape.59), calls=%async_computation.2 | async-start | bytes 589824 | tf_op jit(solution)/shard_map/all_to_all | solution.py:40
  13.7 0.5 copy.89
  14.1 2.0 %reshape.57 = bf16[4,2,18432]{2,1,0:T(2,128)(2,1)} reshape(bf16[128,24,48]{2,1,0:T(8,128)(2,1)S(1)} %bitcast.79) | data formatting | bytes 589824
  16.2 7.1 %all-to-all-done.2 = bf16[4,2,18432]{2,1,0:T(2,128)(2,1)S(1)} async-done(((bf16[4,2,18432]{2,1,0:T(2,128)(2,1)}), bf16[4,2,18432]{2,1,0:T(2,128)(2,1)S(1)}, u32[]{:S(2)}, u32[]{:S(2)}) %all-to-all-start.2) | async-done | bytes 294944 | tf_op jit(solution)/shard_map/all_to_all | solution.py:40
  23.3 3.5 %all-to-all-start = ((bf16[4,2,18432]{2,1,0:T(2,128)(2,1)}), bf16[4,2,18432]{2,1,0:T(2,128)(2,1)S(1)}, u32[]{:S(2)}, u32[]{:S(2)}) async-start(bf16[4,2,18432]{2,1,0:T(2,128)(2,1)} %reshape.57), calls=%async_computation | async-start | bytes 589824 | tf_op jit(solution)/shard_map/all_to_all | solution.py:47
  26.7 0.8 reshape.60
  27.5 0.6 copy.115
  28.1 1.2 %reshape.56 = bf16[192,24,32]{0,1,2:T(8,128)(2,1)} reshape(bf16[4,48,24,32]{1,0,2,3:T(4,128)(2,1)S(1)} %copy.115) | data formatting | bytes 589824 | tf_op jit(solution)/shard_map/all_to_all | solution.py:40
  29.3 5.5 %all-to-all-done = bf16[4,2,18432]{2,1,0:T(2,128)(2,1)S(1)} async-done(((bf16[4,2,18432]{2,1,0:T(2,128)(2,1)}), bf16[4,2,18432]{2,1,0:T(2,128)(2,1)S(1)}, u32[]{:S(2)}, u32[]{:S(2)}) %all-to-all-start) | async-done | bytes 294944 | tf_op jit(solution)/shard_map/all_to_all | solution.py:47
  34.9 3.7 %all-to-all-start.3 = ((bf16[192,24,32]{0,1,2:T(8,128)(2,1)}), bf16[192,24,32]{0,1,2:T(8,128)(2,1)S(1)}, u32[]{:S(2)}, u32[]{:S(2)}) async-start(bf16[192,24,32]{0,1,2:T(8,128)(2,1)} %reshape.56), calls=%async_computation.3 | async-start | bytes 786432 | tf_op jit(solution)/shard_map/all_to_all | solution.py:39
  38.6 0.8 reshape.58
  39.4 0.6 copy.113
  40.0 1.2 %reshape.55 = bf16[192,24,32]{0,1,2:T(8,128)(2,1)} reshape(bf16[4,48,24,32]{1,0,2,3:T(4,128)(2,1)S(1)} %copy.113) | data formatting | bytes 589824 | tf_op jit(solution)/shard_map/all_to_all | solution.py:47
  41.2 4.9 %all-to-all-done.3 = bf16[192,24,32]{0,1,2:T(8,128)(2,1)S(1)} async-done(((bf16[192,24,32]{0,1,2:T(8,128)(2,1)}), bf16[192,24,32]{0,1,2:T(8,128)(2,1)S(1)}, u32[]{:S(2)}, u32[]{:S(2)}) %all-to-all-start.3) | async-done | bytes 294944 | tf_op jit(solution)/shard_map/all_to_all | solution.py:39
  46.0 3.5 %all-to-all-start.1 = ((bf16[192,24,32]{0,1,2:T(8,128)(2,1)}), bf16[192,24,32]{0,1,2:T(8,128)(2,1)S(1)}, u32[]{:S(2)}, u32[]{:S(2)}) async-start(bf16[192,24,32]{0,1,2:T(8,128)(2,1)} %reshape.55), calls=%async_computation.1 | async-start | bytes 786432 | tf_op jit(solution)/shard_map/all_to_all | solution.py:46
  49.5 7.3 %all-to-all-done.1 = bf16[192,24,32]{0,1,2:T(8,128)(2,1)S(1)} async-done(((bf16[192,24,32]{0,1,2:T(8,128)(2,1)}), bf16[192,24,32]{0,1,2:T(8,128)(2,1)S(1)}, u32[]{:S(2)}, u32[]{:S(2)}) %all-to-all-start.1) | async-done | bytes 294944 | tf_op jit(solution)/shard_map/all_to_all | solution.py:46
  56.9 0.3 fusion.12
  57.2 0.3 copy.100
  57.5 14.1 %all_to_all.99 = bf16[192,192,4]{1,2,0:T(4,128)(2,1)S(1)} all-to-all(bf16[192,192,4]{1,2,0:T(4,128)(2,1)S(1)} %copy.100), channel_id=1, replica_groups=mesh['row'=4,'col'=2,'depth'=4] {'row'}, dimensions={0} | all-to-all | bytes 589824 | tf_op jit(solution)/shard_map/all_to_all | solution.py:56
  71.7 0.0 copy-start.6
  71.8 0.7 copy.103
  72.4 1.9 %reshape.61 = bf16[8,2,9216]{2,1,0:T(2,128)(2,1)} reshape(bf16[192,16,48]{2,1,0:T(8,128)(2,1)S(1)} %bitcast.76) | data formatting | bytes 589824
  74.3 3.6 %all-to-all-start.5 = ((bf16[8,2,9216]{2,1,0:T(2,128)(2,1)}), bf16[8,2,9216]{2,1,0:T(2,128)(2,1)S(1)}, u32[]{:S(2)}, u32[]{:S(2)}) async-start(bf16[8,2,9216]{2,1,0:T(2,128)(2,1)} %reshape.61), calls=%async_computation.5 | async-start | bytes 589824 | tf_op jit(solution)/shard_map/all_to_all | solution.py:55
  77.9 0.1 reshape.47
  78.0 0.1 copy.104
  78.1 0.1 copy.105
  78.2 0.1 reshape.48
  78.3 0.1 copy.106
  78.4 0.1 copy.107
  78.6 0.5 fusion.10
  79.1 4.9 %all-to-all-done.5 = bf16[8,2,9216]{2,1,0:T(2,128)(2,1)S(1)} async-done(((bf16[8,2,9216]{2,1,0:T(2,128)(2,1)}), bf16[8,2,9216]{2,1,0:T(2,128)(2,1)S(1)}, u32[]{:S(2)}, u32[]{:S(2)}) %all-to-all-start.5) | async-done | bytes 294944 | tf_op jit(solution)/shard_map/all_to_all | solution.py:55
  84.1 0.8 reshape.62
  84.8 0.2 fusion.1
  85.0 0.3 fusion.4
  85.3 0.4 fusion.7
  85.7 0.2 copy.108
  86.0 0.3 copy.110
  86.3 1.0 %fusion.11 = bf16[48,24,128]{2,1,0:T(8,128)(2,1)} fusion(f32[48,24,128]{2,1,0:T(8,128)S(1)} %fusion.10, bf16[48,24,128]{2,1,0:T(8,128)(2,1)S(1)} %copy.110, bf16[128,128,1]{1,0,2:T(8,128)(2,1)S(1)} %bitcast.86), kind=kOutput, calls=%fused_computation.15 | convolution fusion | flops 38043648 | bytes 1212416 | tf_op jit(solution)/shard_map/xyc,cd->xyd/dot_general | solution.py:70
  (24 shorter events, 0.2 us)
Async XLA Ops:
  0.0 2.9 %copy-start = (bf16[128,512]{1,0:T(8,128)(2,1)S(1)}, bf16[128,512]{1,0:T(8,128)(2,1)}, u32[]{:S(2)}) copy-start(bf16[128,512]{1,0:T(8,128)(2,1)} %param.11) | copy-start | bytes 393220
  7.3 16.0 %all-to-all-start.2 = ((bf16[4,2,18432]{2,1,0:T(2,128)(2,1)}), bf16[4,2,18432]{2,1,0:T(2,128)(2,1)S(1)}, u32[]{:S(2)}, u32[]{:S(2)}) async-start(bf16[4,2,18432]{2,1,0:T(2,128)(2,1)} %reshape.59), calls=%async_computation.2 | async-start | bytes 589824 | tf_op jit(solution)/shard_map/all_to_all | solution.py:40
  23.3 11.6 %all-to-all-start = ((bf16[4,2,18432]{2,1,0:T(2,128)(2,1)}), bf16[4,2,18432]{2,1,0:T(2,128)(2,1)S(1)}, u32[]{:S(2)}, u32[]{:S(2)}) async-start(bf16[4,2,18432]{2,1,0:T(2,128)(2,1)} %reshape.57), calls=%async_computation | async-start | bytes 589824 | tf_op jit(solution)/shard_map/all_to_all | solution.py:47
  34.9 11.2 %all-to-all-start.3 = ((bf16[192,24,32]{0,1,2:T(8,128)(2,1)}), bf16[192,24,32]{0,1,2:T(8,128)(2,1)S(1)}, u32[]{:S(2)}, u32[]{:S(2)}) async-start(bf16[192,24,32]{0,1,2:T(8,128)(2,1)} %reshape.56), calls=%async_computation.3 | async-start | bytes 786432 | tf_op jit(solution)/shard_map/all_to_all | solution.py:39
  46.0 10.8 %all-to-all-start.1 = ((bf16[192,24,32]{0,1,2:T(8,128)(2,1)}), bf16[192,24,32]{0,1,2:T(8,128)(2,1)S(1)}, u32[]{:S(2)}, u32[]{:S(2)}) async-start(bf16[192,24,32]{0,1,2:T(8,128)(2,1)} %reshape.55), calls=%async_computation.1 | async-start | bytes 786432 | tf_op jit(solution)/shard_map/all_to_all | solution.py:46
  71.7 6.3 %copy-start.5 = (f32[128]{0:T(128)S(1)}, f32[128]{0:T(128)}, u32[]{:S(2)}) copy-start(f32[128]{0:T(128)} %param.13) | copy-start | bytes 1540
  71.7 6.5 %copy-start.6 = (f32[128]{0:T(128)S(1)}, f32[128]{0:T(128)}, u32[]{:S(2)}) copy-start(f32[128]{0:T(128)} %param.14) | copy-start | bytes 1540
  71.7 6.8 %copy-start.2 = (bf16[128,128]{1,0:T(8,128)(2,1)S(1)}, bf16[128,128]{1,0:T(8,128)(2,1)}, u32[]{:S(2)}) copy-start(bf16[128,128]{1,0:T(8,128)(2,1)} %param.15) | copy-start | bytes 98308
  71.7 6.8 %copy-start.1 = (bf16[48,24,128]{2,1,0:T(8,128)(2,1)S(1)}, bf16[48,24,128]{2,1,0:T(8,128)(2,1)}, u32[]{:S(2)}) copy-start(bf16[48,24,128]{2,1,0:T(8,128)(2,1)} %param.8) | copy-start | bytes 884740
  71.7 6.8 %copy-start.3 = (f32[128]{0:T(128)S(1)}, f32[128]{0:T(128)}, u32[]{:S(2)}) copy-start(f32[128]{0:T(128)} %param.10) | copy-start | bytes 1540
  71.7 6.8 %copy-start.4 = (f32[128]{0:T(128)S(1)}, f32[128]{0:T(128)}, u32[]{:S(2)}) copy-start(f32[128]{0:T(128)} %param.9) | copy-start | bytes 1540
  71.7 6.8 %copy-start.7 = (bf16[128,128]{1,0:T(8,128)(2,1)S(1)}, bf16[128,128]{1,0:T(8,128)(2,1)}, u32[]{:S(2)}) copy-start(bf16[128,128]{1,0:T(8,128)(2,1)} %param.12) | copy-start | bytes 98308
  74.3 9.7 %all-to-all-start.5 = ((bf16[8,2,9216]{2,1,0:T(2,128)(2,1)}), bf16[8,2,9216]{2,1,0:T(2,128)(2,1)S(1)}, u32[]{:S(2)}, u32[]{:S(2)}) async-start(bf16[8,2,9216]{2,1,0:T(2,128)(2,1)} %reshape.61), calls=%async_computation.5 | async-start | bytes 589824 | tf_op jit(solution)/shard_map/all_to_all | solution.py:55
where the time goes:
time: 88 us; the launch traced here: 87.3 us
  waiting for transfers between devices  29.8 us (34%)
  starting transfers between devices  20.6 us (23%)
  local copies, waits for them, and re-layouts  15.3 us (17%)
  blocking collectives  14.1 us (16%)
  other arithmetic  3.81 us (4%)
  matrix products  3.41 us (4%)
    all_to_all x1, blocking collectives, per_device(): lax.all_to_all(planes.astype(jnp.bfloat16), 'row', split_axis=0, concat_a...  14.1 us
    unnamed x22, local copies, waits for them, and re-layouts  8.3 us
    all_to_all x1, waiting for transfers between devices, per_device(): lax.all_to_all(lax.all_to_all(right_side, 'row', split_axis=2, concat_axi...  7.34 us
    all_to_all x1, waiting for transfers between devices, per_device(): lax.all_to_all(left_side, 'row', split_axis=2, concat_axis=0, tiled=True)  7.1 us
    all_to_all x1, starting transfers between devices, per_device(): lax.all_to_all(left_side, 'row', split_axis=2, concat_axis=0, tiled=True)  6.35 us
    all_to_all x1, waiting for transfers between devices, per_device(): lax.all_to_all(right_side, 'row', split_axis=2, concat_axis=0, tiled=True)  5.54 us
    all_to_all x1, waiting for transfers between devices, per_device(): lax.all_to_all(lax.all_to_all(planes.astype(jnp.bfloat16), 'row', split_a...  4.94 us
    all_to_all x1, waiting for transfers between devices, per_device(): lax.all_to_all(lax.all_to_all(left_side, 'row', split_axis=2, concat_axis...  4.88 us
  transfers between devices with their start and end apart: 5, of which 5 were waited for; matrix products, arithmetic and copies ran while one was open for 10% of the time, Pallas kernels for 0%

commit v1 on v0

v1 whole, which is shorter than its diff:
```python
import functools

import jax
import jax.numpy as jnp
from jax import lax
from jax.experimental import pallas as pl
from jax.experimental.pallas import tpu as pltpu
from jax.sharding import Mesh
from jax.sharding import PartitionSpec as P

LANES = 128
ROWS = 8
NT = (((1,), (1,)), ((), ()))


def layer_norm(values, scaling, offsets):
    average = jnp.mean(values, axis=-1, keepdims=True)
    centred = values - average
    variance = jnp.mean(centred * centred, axis=-1, keepdims=True)
    return centred * lax.rsqrt(variance + 1e-05) * scaling + offsets


def reorder_channels(values, row_count, other_count):
    shape_rest = values.shape[1:]
    grouped = values.reshape((row_count, other_count, -1) + shape_rest)
    return jnp.swapaxes(grouped, 0, 1).reshape(values.shape)


def plain_device(pair_input, in_gain, in_shift, w_proj, w_gate, out_gain, out_shift, w_out):
    row_count = lax.axis_size("row")
    others = ("col", "depth")
    other_count = lax.axis_size("col") * lax.axis_size("depth")
    channels = w_proj.shape[1] // 4
    normed = layer_norm(pair_input.astype(jnp.float32), in_gain, in_shift).astype(jnp.bfloat16)
    projected = jnp.einsum("xyc,cd->xyd", normed, w_proj, preferred_element_type=jnp.float32)
    sides = []
    for at in (0, 2 * channels):
        gate = jax.nn.sigmoid(projected[..., at : at + channels])
        side = (gate * projected[..., at + channels : at + 2 * channels]).astype(jnp.bfloat16)
        side = lax.all_to_all(side, "row", split_axis=2, concat_axis=0, tiled=True)
        sides.append(lax.all_to_all(side, others, split_axis=2, concat_axis=1, tiled=True))
    planes = jnp.einsum("kic,kjc->ijc", *sides, preferred_element_type=jnp.float32)
    product = lax.all_to_all(
        planes.astype(jnp.bfloat16), "row", split_axis=0, concat_axis=2, tiled=True
    )
    product = lax.all_to_all(product, others, split_axis=1, concat_axis=2, tiled=True)
    used = [reorder_channels(a, row_count, other_count) for a in (out_gain, out_shift, w_out)]
    product_norm = layer_norm(product.astype(jnp.float32), used[0], used[1]).astype(jnp.bfloat16)
    gating = jax.nn.sigmoid(
        jnp.einsum("xyc,cd->xyd", normed, w_gate, preferred_element_type=jnp.float32)
    )
    out = jnp.einsum("xyc,cd->xyd", product_norm, used[2], preferred_element_type=jnp.float32)
    return (gating * out).astype(jnp.bfloat16)


def swap_with_lanes(tiles):
    tiles = list(tiles)
    count = len(tiles)
    lane = lax.broadcasted_iota(jnp.int32, tiles[0].shape, 1)
    step = 1
    while step < count:
        upper = (lane & step) != 0
        new = list(tiles)
        for v in range(count):
            if not v & step:
                low, high = tiles[v], tiles[v | step]
                new[v] = jnp.where(upper, pltpu.roll(high, step, 1), low)
                new[v | step] = jnp.where(upper, high, pltpu.roll(low, LANES - step, 1))
        tiles = new
        step *= 2
    return tiles


def side_of(normed, weights, channels):
    projected = jnp.dot(normed, weights, preferred_element_type=jnp.float32)
    return jax.nn.sigmoid(projected[:, :channels]) * projected[:, channels:]


def store_side(side, out_ref, split, k_group, i_tile):
    tiles = [side[s * ROWS : (s + 1) * ROWS] for s in range(split)]
    tiles = swap_with_lanes(tiles)
    for s in range(split):
        out_ref[
            s,
            i_tile * ROWS : (i_tile + 1) * ROWS,
            k_group * LANES : (k_group + 1) * LANES,
        ] = tiles[s].astype(out_ref.dtype)


def left_kernel(split, x_ref, gain_ref, shift_ref, w_ref, normed_ref, out_ref):
    rows, columns, channels = x_ref.shape
    for k_group in range(rows // split):
        for i_tile in range(columns // ROWS):
            at = (slice(k_group * split, (k_group + 1) * split), slice(i_tile * ROWS, (i_tile + 1) * ROWS))
            values = x_ref[at].astype(jnp.float32).reshape(split * ROWS, channels)
            normed = layer_norm(values, gain_ref[...], shift_ref[...])
            normed_ref[at] = normed.reshape(split, ROWS, channels).astype(jnp.bfloat16)
            side = side_of(normed.astype(jnp.bfloat16), w_ref[:, : 2 * channels], channels)
            store_side(side, out_ref, split, k_group, i_tile)


def right_kernel(split, normed_ref, w_ref, out_ref):
    rows, columns, channels = normed_ref.shape
    for k_group in range(rows // split):
        for i_tile in range(columns // ROWS):
            at = (slice(k_group * split, (k_group + 1) * split), slice(i_tile * ROWS, (i_tile + 1) * ROWS))
            normed = normed_ref[at].reshape(split * ROWS, channels)
            side = side_of(normed, w_ref[:, 2 * channels :], channels)
            store_side(side, out_ref, split, k_group, i_tile)


def gate_kernel(normed_ref, w_ref, out_ref):
    rows, columns, channels = normed_ref.shape
    normed = normed_ref[...].reshape(rows * columns, channels)
    gate = jax.nn.sigmoid(jnp.dot(normed, w_ref[...], preferred_element_type=jnp.float32))
    out_ref[...] = gate.reshape(rows, columns, channels)


def product_kernel(split, own_ref, other_ref, right_ref, out_ref):
    row_count, rows, width = own_ref.shape
    columns = rows // row_count
    groups = LANES // split
    right = jnp.concatenate([right_ref[r] for r in range(row_count)], axis=1)
    lane = lax.broadcasted_iota(jnp.int32, (split, row_count * width), 1)
    group = lax.rem(lane, LANES) // split
    for target in range(row_count):
        at = slice(target * columns, (target + 1) * columns)
        left = jnp.concatenate(
            [
                jnp.concatenate([ref[r, at, :] for r in range(row_count)], axis=1)
                for ref in (own_ref, other_ref)
            ],
            axis=0,
        )
        parts = []
        for slab in range(2 * columns // split):
            piece = left[slab * split : (slab + 1) * split]
            for g in range(groups):
                parts.append(jnp.where(group == g, piece, jnp.zeros_like(piece)))
        masked = jnp.concatenate(parts, axis=0)
        block = lax.dot_general(right, masked, NT, preferred_element_type=jnp.float32)
        out_ref[target] = block.astype(out_ref.dtype)


def output_kernel(split, place_ref, sums_ref, gate_ref, gain_ref, shift_ref, w_ref, out_ref):
    _, columns, width = sums_ref.shape
    rows, _, channels = out_ref.shape
    parity = place_ref[0]
    pieces = split // ROWS
    for j_tile in range(columns // ROWS):
        js = slice(j_tile * ROWS, (j_tile + 1) * ROWS)
        for slab in range(width // LANES):
            lanes = slice(slab * LANES, (slab + 1) * LANES)
            tiles = [sums_ref[s, js, lanes].astype(jnp.float32) for s in range(split)]
            tiles = swap_with_lanes(tiles)
            values = jnp.concatenate(tiles, axis=0)
            normed = layer_norm(values, gain_ref[...], shift_ref[...]).astype(jnp.bfloat16)
            projected = jnp.dot(normed, w_ref[...], preferred_element_type=jnp.float32)
            for piece in range(pieces):
                first = slab * split + piece * ROWS
                half, rest = divmod(first, rows // 2)
                block, inside = divmod(rest, columns)
                core = parity if half == 0 else 1 - parity
                at = pl.ds((2 * block + core) * columns + inside, ROWS)
                value = projected[piece * ROWS * ROWS : (piece + 1) * ROWS * ROWS]
                value = value.reshape(ROWS, ROWS, channels)
                out_ref[at, js, :] = (gate_ref[at, js, :] * value).astype(out_ref.dtype)


def call(kernel, name, out_shape, flops, *arrays, scalars=0):
    specs = [pl.BlockSpec(memory_space=pltpu.SMEM)] * scalars
    specs += [pl.BlockSpec(memory_space=pltpu.VMEM)] * (len(arrays) - scalars)
    outs = jax.tree.leaves(out_shape)
    moved = sum(a.size * a.dtype.itemsize for a in [*arrays, *outs])
    return pl.pallas_call(
        kernel,
        name=name,
        out_shape=out_shape,
        in_specs=specs,
        out_specs=jax.tree.map(lambda _: pl.BlockSpec(memory_space=pltpu.VMEM), out_shape),
        cost_estimate=pl.CostEstimate(flops=flops, bytes_accessed=moved, transcendentals=0),
    )(*arrays)


def fast_device(pair_input, in_gain, in_shift, w_proj, w_gate, out_gain, out_shift, w_out):
    rows, columns, channels = pair_input.shape
    row_count = lax.axis_size("row")
    owners = ("row", "col", "depth")
    split = row_count * lax.axis_size("col") * lax.axis_size("depth")
    width = rows // split * LANES
    per_row = split // row_count
    bf16 = jnp.bfloat16
    gains = [a.reshape(1, channels) for a in (in_gain, in_shift, out_gain, out_shift)]
    message = jax.ShapeDtypeStruct((split, columns, width), bf16)
    flops = 4 * rows * columns * channels * channels

    normed, left = call(
        functools.partial(left_kernel, split),
        "left",
        (jax.ShapeDtypeStruct(pair_input.shape, bf16), message),
        flops,
        pair_input,
        gains[0],
        gains[1],
        w_proj,
    )
    exchange = functools.partial(
        lax.all_to_all, axis_name=owners, split_axis=0, concat_axis=0, tiled=True
    )
    own = exchange(left)
    right = exchange(call(functools.partial(right_kernel, split), "right", message, flops, normed, w_proj))
    gate = call(gate_kernel, "gate", jax.ShapeDtypeStruct(pair_input.shape, jnp.float32), flops // 2, normed, w_gate)
    other = lax.ppermute(own, "core", [(0, 1), (1, 0)])
    stacked = (row_count, per_row * columns, width)
    sums = call(
        functools.partial(product_kernel, split),
        "product",
        jax.ShapeDtypeStruct(stacked, bf16),
        flops,
        own.reshape(stacked),
        other.reshape(stacked),
        right.reshape(stacked),
    )
    sums = exchange(sums.reshape(message.shape))
    place = lax.axis_index("core").astype(jnp.int32).reshape(1)
    return call(
        functools.partial(output_kernel, split),
        "output",
        jax.ShapeDtypeStruct(pair_input.shape, bf16),
        flops // 2,
        place,
        sums,
        gate,
        gains[2],
        gains[3],
        w_out,
        scalars=1,
    )


def suits(mesh, pair_input, w_proj):
    row_count, col_count, depth_count = (mesh.shape[a] for a in ("row", "col", "depth"))
    split = row_count * col_count * depth_count // 2
    rows, columns = pair_input.shape[0] // row_count, pair_input.shape[1] // (col_count * depth_count)
    return (
        depth_count % 2 == 0
        and pair_input.shape[0] == pair_input.shape[1]
        and pair_input.shape[2] == LANES
        and w_proj.shape == (LANES, 4 * LANES)
        and split & (split - 1) == 0
        and split >= 16
        and LANES % split == 0
        and rows % split == 0
        and columns % ROWS == 0
        and rows % (2 * columns) == 0
    )


def solution(mesh):
    def step(pair_input, in_gain, in_shift, w_proj, w_gate, out_gain, out_shift, w_out):
        if suits(mesh, pair_input, w_proj):
            row_count, col_count, depth_count = mesh.devices.shape
            used = Mesh(
                mesh.devices.reshape(row_count, col_count, depth_count // 2, 2),
                ("row", "col", "depth", "core"),
            )
            pair, body = P("row", ("col", "depth", "core"), None), fast_device
        else:
            used, pair, body = mesh, P("row", ("col", "depth"), None), plain_device
        return jax.shard_map(
            body,
            mesh=used,
            in_specs=(pair, P(), P(), P(), P(), P(), P(), P()),
            out_specs=pair,
            check_vma=False,
        )(pair_input, in_gain, in_shift, w_proj, w_gate, out_gain, out_shift, w_out)

    return step
```

time: 88 us -> 58.9 us (0.67)
  Pallas kernels: 0 us -> 15.2 us
  blocking collectives: 14.1 us -> 0 us
  local copies, waits for them, and re-layouts: 15.3 us -> 1.54 us
  starting transfers between devices: 20.6 us -> 15.5 us
  other arithmetic: 3.81 us -> 0 us
  waiting for transfers between devices: 29.8 us -> 26.1 us
  matrix products: 3.41 us -> 0 us
    pallas_call x0 -> x5, Pallas kernels: none -> 15.2 us  [call(): pl.pallas_call(kernel, name=name, out_shape=out_shape, in_specs=specs, ou...]
    all_to_all x1 -> x0, blocking collectives: 14.1 us -> none  [per_device(): lax.all_to_all(planes.astype(jnp.bfloat16), 'row', split_axis=0, concat_a...]
    unnamed x22 -> x8, local copies, waits for them, and re-layouts: 8.3 us -> 1.54 us
    all_to_all x5 -> x3, starting transfers between devices: 20.6 us -> 15.4 us  [the longest x1 8.34 us: fast_device(): own = exchange(left)]
    all_to_all x9 -> x0, local copies, waits for them, and re-layouts: 4.36 us -> none  [the longest x2 1.8 us: per_device(): lax.all_to_all(left_side, 'row', split_axis=2, concat_axis=0, tiled=True)]
    all_to_all x5 -> x3, waiting for transfers between devices: 29.8 us -> 26 us  [the longest x1 9.86 us: fast_device(): exchange(call(functools.partial(right_kernel, split), 'right', message, f...]
    dot_general x4 -> x0, matrix products: 3.41 us -> none  [the longest x1 1.56 us: gated_sides(): jnp.einsum('xyc,cd->xyd', normed, w_proj, preferred_element_type=jnp.floa...]
    reduce_sum x4 -> x0, other arithmetic: 3.05 us -> none  [the longest x2 1.65 us: layer_norm(): variance = jnp.mean(centred * centred, axis=-1, keepdims=True)]
  transfers between devices with their start and end apart: 5 -> 4, of which waited for: 5 -> 3; matrix products, arithmetic and copies ran while one was open for 10% -> 0% of each run, Pallas kernels for 0% -> 7%
where the time goes in v1:
time: 58.9 us; the launch traced here: 58.4 us
  waiting for transfers between devices  26.1 us (44%)
  starting transfers between devices  15.5 us (26%)
  Pallas kernels  15.2 us (26%)
  local copies, waits for them, and re-layouts  1.54 us (3%)
    pallas_call x5, Pallas kernels, call(): pl.pallas_call(kernel, name=name, out_shape=out_shape, in_specs=specs, ou...  15.2 us
    all_to_all x1, waiting for transfers between devices, fast_device(): exchange(call(functools.partial(right_kernel, split), 'right', message, f...  9.86 us
    all_to_all x1, starting transfers between devices, fast_device(): own = exchange(left)  8.34 us
    all_to_all x1, waiting for transfers between devices, fast_device(): own = exchange(left)  8.33 us
    all_to_all x1, waiting for transfers between devices, fast_device(): sums = exchange(sums.reshape(message.shape))  7.86 us
    all_to_all x1, starting transfers between devices, fast_device(): exchange(call(functools.partial(right_kernel, split), 'right', message, f...  3.54 us
    all_to_all x1, starting transfers between devices, fast_device(): sums = exchange(sums.reshape(message.shape))  3.54 us
    unnamed x8, local copies, waits for them, and re-layouts  1.54 us
  transfers between devices with their start and end apart: 4, of which 3 were waited for; matrix products, arithmetic and copies ran while one was open for 0% of the time, Pallas kernels for 7%

profile of v1, /device:TPU:0, one launch (start us, length us, event | category | flops | bytes accessed | tf_op | source)
XLA Modules:
  0.0 58.4 jit_solution(4928065482880544180)
XLA Ops:
  0.0 3.8 %left.1 = (bf16[48,24,128]{2,1,0:T(8,128)(2,1)}, bf16[16,24,384]{2,1,0:T(8,128)(2,1)}) custom-call(bf16[48,24,128]{2,1,0:T(8,128)(2,1)} %x_ref.1, f32[1,128]{1,0:T(1,128)} %bitcast.15, f32[1,128]{1,0:T(1,128)} %bitcast.16, bf16[128,512]{1,0:T(8,128)(2,1)} %w_ref.5), custom_call_target="tpu_custom_call" | custom-call | flops 75497472 | bytes 1016832 | tf_op jit(solution)/shard_map/left/pallas_call | solution.py:175
  3.8 8.3 %all-to-all-start = ((bf16[16,24,384]{2,1,0:T(8,128)(2,1)}), bf16[16,24,384]{2,1,0:T(8,128)(2,1)S(1)}, u32[]{:S(2)}, u32[]{:S(2)}) async-start(bf16[16,24,384]{2,1,0:T(8,128)(2,1)} %get-tuple-element.7), calls=%async_computation | async-start | bytes 589824 | tf_op jit(solution)/shard_map/all_to_all | solution.py:210
  12.2 2.4 %right.1 = bf16[16,24,384]{2,1,0:T(8,128)(2,1)} custom-call(bf16[48,24,128]{2,1,0:T(8,128)(2,1)} %get-tuple-element.8.normed_ref, bf16[128,512]{1,0:T(8,128)(2,1)} %w_ref.5), custom_call_target="tpu_custom_call" | custom-call | flops 75497472 | bytes 720896 | tf_op jit(solution)/shard_map/right/pallas_call | solution.py:175
  14.5 8.3 %all-to-all-done = bf16[16,24,384]{2,1,0:T(8,128)(2,1)S(1)} async-done(((bf16[16,24,384]{2,1,0:T(8,128)(2,1)}), bf16[16,24,384]{2,1,0:T(8,128)(2,1)S(1)}, u32[]{:S(2)}, u32[]{:S(2)}) %all-to-all-start) | async-done | bytes 294944 | tf_op jit(solution)/shard_map/all_to_all | solution.py:210
  22.9 0.0 copy-start.1
  22.9 3.5 %all-to-all-start.1 = ((bf16[16,24,384]{2,1,0:T(8,128)(2,1)}), bf16[16,24,384]{2,1,0:T(8,128)(2,1)S(1)}, u32[]{:S(2)}, u32[]{:S(2)}) async-start(bf16[16,24,384]{2,1,0:T(8,128)(2,1)} %right.1), calls=%async_computation.1 | async-start | bytes 589824 | tf_op jit(solution)/shard_map/all_to_all | solution.py:211
  26.4 0.1 collective-permute-start
  26.5 9.9 %all-to-all-done.1 = bf16[16,24,384]{2,1,0:T(8,128)(2,1)S(1)} async-done(((bf16[16,24,384]{2,1,0:T(8,128)(2,1)}), bf16[16,24,384]{2,1,0:T(8,128)(2,1)S(1)}, u32[]{:S(2)}, u32[]{:S(2)}) %all-to-all-start.1) | async-done | bytes 294944 | tf_op jit(solution)/shard_map/all_to_all | solution.py:211
  36.3 0.0 copy-start.2
  36.4 0.0 collective-permute-done
  36.4 0.0 copy-start.3
  36.4 0.0 copy-done.1
  36.4 0.7 %copy-done.2 = bf16[16,24,384]{2,1,0:T(8,128)(2,1)} copy-done((bf16[16,24,384]{2,1,0:T(8,128)(2,1)}, bf16[16,24,384]{2,1,0:T(8,128)(2,1)S(1)}, u32[]{:S(2)}) %copy-start.2) | copy-done | bytes 294936
  37.1 0.1 copy-done.3
  37.2 3.4 %product.1 = bf16[4,96,384]{2,1,0:T(8,128)(2,1)} custom-call(bf16[4,96,384]{2,1,0:T(8,128)(2,1)} %bitcast.9, bf16[4,96,384]{2,1,0:T(8,128)(2,1)} %bitcast.12, bf16[4,96,384]{2,1,0:T(8,128)(2,1)} %bitcast.10), custom_call_target="tpu_custom_call" | custom-call | flops 75497472 | bytes 1179648 | tf_op jit(solution)/shard_map/product/pallas_call | solution.py:175
  40.5 3.5 %all-to-all-start.2 = ((bf16[16,24,384]{2,1,0:T(8,128)(2,1)}), bf16[16,24,384]{2,1,0:T(8,128)(2,1)S(1)}, u32[]{:S(2)}, u32[]{:S(2)}) async-start(bf16[16,24,384]{2,1,0:T(8,128)(2,1)} %bitcast.11), calls=%async_computation.2 | async-start | bytes 589824 | tf_op jit(solution)/shard_map/all_to_all | solution.py:224
  44.1 2.0 %gate.1.gate_ref = f32[48,24,128]{2,1,0:T(8,128)} custom-call(bf16[48,24,128]{2,1,0:T(8,128)(2,1)} %get-tuple-element.8.normed_ref, bf16[128,128]{1,0:T(8,128)(2,1)} %w_ref.6), custom_call_target="tpu_custom_call" | custom-call | flops 37748736 | bytes 917504 | tf_op jit(solution)/shard_map/gate/pallas_call | solution.py:175
  46.1 7.9 %all-to-all-done.2.sums_ref = bf16[16,24,384]{2,1,0:T(8,128)(2,1)S(1)} async-done(((bf16[16,24,384]{2,1,0:T(8,128)(2,1)}), bf16[16,24,384]{2,1,0:T(8,128)(2,1)S(1)}, u32[]{:S(2)}, u32[]{:S(2)}) %all-to-all-start.2) | async-done | bytes 294944 | tf_op jit(solution)/shard_map/all_to_all | solution.py:224
  54.0 0.0 copy-start
  54.0 0.7 %copy-done = bf16[16,24,384]{2,1,0:T(8,128)(2,1)} copy-done((bf16[16,24,384]{2,1,0:T(8,128)(2,1)}, bf16[16,24,384]{2,1,0:T(8,128)(2,1)S(1)}, u32[]{:S(2)}) %copy-start) | copy-done | bytes 294936
  54.7 3.7 %output.1 = bf16[48,24,128]{2,1,0:T(8,128)(2,1)} custom-call(s32[1]{0:T(128)} %bitcast.place_ref, bf16[16,24,384]{2,1,0:T(8,128)(2,1)} %copy-done, f32[48,24,128]{2,1,0:T(8,128)} %gate.1.gate_ref, f32[1,128]{1,0:T(1,128)} %bitcast.13, f32[1,128]{1,0:T(1,128)} %bitcast.14, bf16[128,128]{1,0:T(8,128)(2,1)} %w_ref.7), custom_call_target="tpu_custom_call" | custom-call | flops 37748736 | bytes 1213444 | tf_op jit(solution)/shard_map/output/pallas_call | solution.py:175
Async XLA Ops:
  3.8 19.0 %all-to-all-start = ((bf16[16,24,384]{2,1,0:T(8,128)(2,1)}), bf16[16,24,384]{2,1,0:T(8,128)(2,1)S(1)}, u32[]{:S(2)}, u32[]{:S(2)}) async-start(bf16[16,24,384]{2,1,0:T(8,128)(2,1)} %get-tuple-element.7), calls=%async_computation | async-start | bytes 589824 | tf_op jit(solution)/shard_map/all_to_all | solution.py:210
  22.9 13.5 %copy-start.1 = (bf16[16,24,384]{2,1,0:T(8,128)(2,1)}, bf16[16,24,384]{2,1,0:T(8,128)(2,1)S(1)}, u32[]{:S(2)}) copy-start(bf16[16,24,384]{2,1,0:T(8,128)(2,1)S(1)} %all-to-all-done) | copy-start | bytes 884740
  22.9 13.5 %all-to-all-start.1 = ((bf16[16,24,384]{2,1,0:T(8,128)(2,1)}), bf16[16,24,384]{2,1,0:T(8,128)(2,1)S(1)}, u32[]{:S(2)}, u32[]{:S(2)}) async-start(bf16[16,24,384]{2,1,0:T(8,128)(2,1)} %right.1), calls=%async_computation.1 | async-start | bytes 589824 | tf_op jit(solution)/shard_map/all_to_all | solution.py:211
  26.4 9.9 %collective-permute-start = (bf16[16,24,384]{2,1,0:T(8,128)(2,1)S(1)}, bf16[16,24,384]{2,1,0:T(8,128)(2,1)S(1)}, u32[]{:S(2)}, u32[]{:S(2)}) collective-permute-start(bf16[16,24,384]{2,1,0:T(8,128)(2,1)S(1)} %all-to-all-done), channel_id=1, source_target_pairs={{0,1},{1,0},{2,3},{3,2},{4,5},{5,4},{6,7},{7,6},{8,9},{9,8},{10,11... | collective-permute-start | bytes 884744 | tf_op jit(solution)/shard_map/ppermute | solution.py:213
  36.3 0.7 %copy-start.2 = (bf16[16,24,384]{2,1,0:T(8,128)(2,1)}, bf16[16,24,384]{2,1,0:T(8,128)(2,1)S(1)}, u32[]{:S(2)}) copy-start(bf16[16,24,384]{2,1,0:T(8,128)(2,1)S(1)} %all-to-all-done.1) | copy-start | bytes 884740
  36.4 0.8 %copy-start.3 = (bf16[16,24,384]{2,1,0:T(8,128)(2,1)}, bf16[16,24,384]{2,1,0:T(8,128)(2,1)S(1)}, u32[]{:S(2)}) copy-start(bf16[16,24,384]{2,1,0:T(8,128)(2,1)S(1)} %collective-permute-done) | copy-start | bytes 884740
  40.5 13.4 %all-to-all-start.2 = ((bf16[16,24,384]{2,1,0:T(8,128)(2,1)}), bf16[16,24,384]{2,1,0:T(8,128)(2,1)S(1)}, u32[]{:S(2)}, u32[]{:S(2)}) async-start(bf16[16,24,384]{2,1,0:T(8,128)(2,1)} %bitcast.11), calls=%async_computation.2 | async-start | bytes 589824 | tf_op jit(solution)/shard_map/all_to_all | solution.py:224
  54.0 0.7 %copy-start = (bf16[16,24,384]{2,1,0:T(8,128)(2,1)}, bf16[16,24,384]{2,1,0:T(8,128)(2,1)S(1)}, u32[]{:S(2)}) copy-start(bf16[16,24,384]{2,1,0:T(8,128)(2,1)S(1)} %all-to-all-done.2.sums_ref) | copy-start | bytes 884740

commit v2 on v1

--- a/solution.py
+++ b/solution.py
@@ -10,6 +10,7 @@
 
 LANES = 128
 ROWS = 8
+VMEM_LIMIT = 24 * 1024 * 1024
 NT = (((1,), (1,)), ((), ()))
 
 
@@ -179,6 +180,7 @@
         in_specs=specs,
         out_specs=jax.tree.map(lambda _: pl.BlockSpec(memory_space=pltpu.VMEM), out_shape),
         cost_estimate=pl.CostEstimate(flops=flops, bytes_accessed=moved, transcendentals=0),
+        compiler_params=pltpu.CompilerParams(vmem_limit_bytes=VMEM_LIMIT),
     )(*arrays)
 
 

time: 58.9 us -> 57.5 us (0.976)
  Pallas kernels: 15.2 us -> 9.2 us
  waiting for transfers between devices: 26.1 us -> 28.8 us
  local copies, waits for them, and re-layouts: 1.54 us -> 3.22 us
    pallas_call x5, Pallas kernels: 15.2 us -> 9.2 us  [call(): pl.pallas_call(kernel, name=name, out_shape=out_shape, in_specs=specs, ou...]
    all_to_all x1, waiting for transfers between devices: 7.86 us -> 9.6 us  [fast_device(): sums = exchange(sums.reshape(message.shape))]
    unnamed x8 -> x18, local copies, waits for them, and re-layouts: 1.54 us -> 3.22 us
    all_to_all x1, waiting for transfers between devices: 8.33 us -> 9.32 us  [fast_device(): own = exchange(left)]
  transfers between devices with their start and end apart: 4 -> 4, of which waited for: 3 -> 3; matrix products, arithmetic and copies ran while one was open for 0% -> 0% of each run, Pallas kernels for 7% -> 3%
where the time goes in v2:
time: 57.5 us; the launch traced here: 57 us
  waiting for transfers between devices  28.8 us (50%)
  starting transfers between devices  15.8 us (27%)
  Pallas kernels  9.2 us (16%)
  local copies, waits for them, and re-layouts  3.22 us (6%)
    all_to_all x1, waiting for transfers between devices, fast_device(): exchange(call(functools.partial(right_kernel, split), 'right', message, f...  9.86 us
    all_to_all x1, waiting for transfers between devices, fast_device(): sums = exchange(sums.reshape(message.shape))  9.6 us
    all_to_all x1, waiting for transfers between devices, fast_device(): own = exchange(left)  9.32 us
    pallas_call x5, Pallas kernels, call(): pl.pallas_call(kernel, name=name, out_shape=out_shape, in_specs=specs, ou...  9.2 us
    all_to_all x1, starting transfers between devices, fast_device(): own = exchange(left)  8.47 us
    all_to_all x1, starting transfers between devices, fast_device(): sums = exchange(sums.reshape(message.shape))  3.67 us
    all_to_all x1, starting transfers between devices, fast_device(): exchange(call(functools.partial(right_kernel, split), 'right', message, f...  3.54 us
    unnamed x18, local copies, waits for them, and re-layouts  3.22 us
  transfers between devices with their start and end apart: 4, of which 3 were waited for; matrix products, arithmetic and copies ran while one was open for 0% of the time, Pallas kernels for 3%

profile of v2, /device:TPU:0, one launch (start us, length us, event | category | flops | bytes accessed | tf_op | source)
XLA Modules:
  0.0 57.0 jit_solution(6446083763682767661)
XLA Ops:
  0.0 0.0 copy-start.7
  0.0 0.0 copy-start.8
  0.0 0.7 %copy-done.7 = f32[128]{0:T(128)S(1)} copy-done((f32[128]{0:T(128)S(1)}, f32[128]{0:T(128)}, u32[]{:S(2)}) %copy-start.7) | copy-done | bytes 536
  0.7 0.0 copy-done.8
  0.7 0.0 copy-start
  0.7 0.9 %copy-done = bf16[128,512]{1,0:T(8,128)(2,1)S(1)} copy-done((bf16[128,512]{1,0:T(8,128)(2,1)S(1)}, bf16[128,512]{1,0:T(8,128)(2,1)}, u32[]{:S(2)}) %copy-start) | copy-done | bytes 131096
  1.6 0.0 copy-start.2
  1.6 1.0 %copy-done.2 = bf16[48,24,128]{2,1,0:T(8,128)(2,1)S(1)} copy-done((bf16[48,24,128]{2,1,0:T(8,128)(2,1)S(1)}, bf16[48,24,128]{2,1,0:T(8,128)(2,1)}, u32[]{:S(2)}) %copy-start.2) | copy-done | bytes 294936
  2.5 2.8 %left.1 = (bf16[48,24,128]{2,1,0:T(8,128)(2,1)S(1)}, bf16[16,24,384]{2,1,0:T(8,128)(2,1)}) custom-call(bf16[48,24,128]{2,1,0:T(8,128)(2,1)S(1)} %copy-done.2, f32[1,128]{1,0:T(1,128)S(1)} %bitcast.14, f32[1,128]{1,0:T(1,128)S(1)} %bitcast.15, bf16[128,512]{1,0:T(8,128)(2,1)S(1)} %copy-done), custom_call_target="tpu_custom_call" | custom-call | flops 75497472 | bytes 1016832 | tf_op jit(solution)/shard_map/left/pallas_call | solution.py:176
  5.4 0.0 copy-start.1
  5.4 8.5 %all-to-all-start = ((bf16[16,24,384]{2,1,0:T(8,128)(2,1)}), bf16[16,24,384]{2,1,0:T(8,128)(2,1)S(1)}, u32[]{:S(2)}, u32[]{:S(2)}) async-start(bf16[16,24,384]{2,1,0:T(8,128)(2,1)} %get-tuple-element.7), calls=%async_computation | async-start | bytes 589824 | tf_op jit(solution)/shard_map/all_to_all | solution.py:212
  13.9 0.0 copy-done.1
  13.9 1.4 %right.1 = bf16[16,24,384]{2,1,0:T(8,128)(2,1)} custom-call(bf16[48,24,128]{2,1,0:T(8,128)(2,1)S(1)} %get-tuple-element.8.normed_ref, bf16[128,512]{1,0:T(8,128)(2,1)S(1)} %copy-done.1), custom_call_target="tpu_custom_call" | custom-call | flops 75497472 | bytes 720896 | tf_op jit(solution)/shard_map/right/pallas_call | solution.py:176
  15.2 9.3 %all-to-all-done = bf16[16,24,384]{2,1,0:T(8,128)(2,1)S(1)} async-done(((bf16[16,24,384]{2,1,0:T(8,128)(2,1)}), bf16[16,24,384]{2,1,0:T(8,128)(2,1)S(1)}, u32[]{:S(2)}, u32[]{:S(2)}) %all-to-all-start) | async-done | bytes 294944 | tf_op jit(solution)/shard_map/all_to_all | solution.py:212
  24.5 3.5 %all-to-all-start.1 = ((bf16[16,24,384]{2,1,0:T(8,128)(2,1)}), bf16[16,24,384]{2,1,0:T(8,128)(2,1)S(1)}, u32[]{:S(2)}, u32[]{:S(2)}) async-start(bf16[16,24,384]{2,1,0:T(8,128)(2,1)} %right.1), calls=%async_computation.1 | async-start | bytes 589824 | tf_op jit(solution)/shard_map/all_to_all | solution.py:213
  28.1 0.1 collective-permute-start
  28.2 9.9 %all-to-all-done.1 = bf16[16,24,384]{2,1,0:T(8,128)(2,1)S(1)} async-done(((bf16[16,24,384]{2,1,0:T(8,128)(2,1)}), bf16[16,24,384]{2,1,0:T(8,128)(2,1)S(1)}, u32[]{:S(2)}, u32[]{:S(2)}) %all-to-all-start.1) | async-done | bytes 294944 | tf_op jit(solution)/shard_map/all_to_all | solution.py:213
  38.0 0.0 collective-permute-done
  38.0 2.2 %product.1 = bf16[4,96,384]{2,1,0:T(8,128)(2,1)} custom-call(bf16[4,96,384]{2,1,0:T(8,128)(2,1)S(1)} %bitcast.9, bf16[4,96,384]{2,1,0:T(8,128)(2,1)S(1)} %bitcast.11, bf16[4,96,384]{2,1,0:T(8,128)(2,1)S(1)} %bitcast.10), custom_call_target="tpu_custom_call" | custom-call | flops 75497472 | bytes 1179648 | tf_op jit(solution)/shard_map/product/pallas_call | solution.py:176
  40.3 0.0 copy-start.3
  40.3 3.7 %all-to-all-start.2 = ((bf16[16,24,384]{2,1,0:T(8,128)(2,1)}), bf16[16,24,384]{2,1,0:T(8,128)(2,1)S(1)}, u32[]{:S(2)}, u32[]{:S(2)}) async-start(bf16[16,24,384]{2,1,0:T(8,128)(2,1)} %bitcast.6), calls=%async_computation.2 | async-start | bytes 589824 | tf_op jit(solution)/shard_map/all_to_all | solution.py:226
  44.0 0.0 copy-done.3
  44.0 0.0 copy-start.4
  44.0 0.2 gate.1.gate_ref
  44.2 9.6 %all-to-all-done.2.sums_ref = bf16[16,24,384]{2,1,0:T(8,128)(2,1)S(1)} async-done(((bf16[16,24,384]{2,1,0:T(8,128)(2,1)}), bf16[16,24,384]{2,1,0:T(8,128)(2,1)S(1)}, u32[]{:S(2)}, u32[]{:S(2)}) %all-to-all-start.2) | async-done | bytes 294944 | tf_op jit(solution)/shard_map/all_to_all | solution.py:226
  53.8 0.0 copy-start.5
  53.8 0.0 copy-start.6
  53.8 0.0 copy-done.4
  53.8 0.6 %copy-done.5 = f32[128]{0:T(128)S(1)} copy-done((f32[128]{0:T(128)S(1)}, f32[128]{0:T(128)}, u32[]{:S(2)}) %copy-start.5) | copy-done | bytes 536
  54.5 0.0 copy-done.6
  54.5 2.5 %output.1 = bf16[48,24,128]{2,1,0:T(8,128)(2,1)} custom-call(s32[1]{0:T(128)} %bitcast.place_ref, bf16[16,24,384]{2,1,0:T(8,128)(2,1)S(1)} %all-to-all-done.2.sums_ref, f32[48,24,128]{2,1,0:T(8,128)S(1)} %gate.1.gate_ref, f32[1,128]{1,0:T(1,128)S(1)} %bitcast.12, f32[1,128]{1,0:T(1,128)S(1)} %bitcast.13, bf16[128,128]{1,0:T(8,128)(2,1)S(1)} %copy-done.4), custom_call_target="tpu_custom_call" | custom-call | flops 37748736 | bytes 1213444 | tf_op jit(solution)/shard_map/output/pallas_call | solution.py:176
Async XLA Ops:
  0.0 0.7 %copy-start.7 = (f32[128]{0:T(128)S(1)}, f32[128]{0:T(128)}, u32[]{:S(2)}) copy-start(f32[128]{0:T(128)} %param.9) | copy-start | bytes 1540
  0.0 0.7 %copy-start.8 = (f32[128]{0:T(128)S(1)}, f32[128]{0:T(128)}, u32[]{:S(2)}) copy-start(f32[128]{0:T(128)} %param.10) | copy-start | bytes 1540
  0.7 0.9 %copy-start = (bf16[128,512]{1,0:T(8,128)(2,1)S(1)}, bf16[128,512]{1,0:T(8,128)(2,1)}, u32[]{:S(2)}) copy-start(bf16[128,512]{1,0:T(8,128)(2,1)} %w_ref.5) | copy-start | bytes 393220
  1.6 1.0 %copy-start.2 = (bf16[48,24,128]{2,1,0:T(8,128)(2,1)S(1)}, bf16[48,24,128]{2,1,0:T(8,128)(2,1)}, u32[]{:S(2)}) copy-start(bf16[48,24,128]{2,1,0:T(8,128)(2,1)} %x_ref.1) | copy-start | bytes 884740
  5.4 8.5 %copy-start.1 = (bf16[128,512]{1,0:T(8,128)(2,1)S(1)}, bf16[128,512]{1,0:T(8,128)(2,1)}, u32[]{:S(2)}) copy-start(bf16[128,512]{1,0:T(8,128)(2,1)} %w_ref.5) | copy-start | bytes 393220
  5.4 19.2 %all-to-all-start = ((bf16[16,24,384]{2,1,0:T(8,128)(2,1)}), bf16[16,24,384]{2,1,0:T(8,128)(2,1)S(1)}, u32[]{:S(2)}, u32[]{:S(2)}) async-start(bf16[16,24,384]{2,1,0:T(8,128)(2,1)} %get-tuple-element.7), calls=%async_computation | async-start | bytes 589824 | tf_op jit(solution)/shard_map/all_to_all | solution.py:212
  24.5 13.5 %all-to-all-start.1 = ((bf16[16,24,384]{2,1,0:T(8,128)(2,1)}), bf16[16,24,384]{2,1,0:T(8,128)(2,1)S(1)}, u32[]{:S(2)}, u32[]{:S(2)}) async-start(bf16[16,24,384]{2,1,0:T(8,128)(2,1)} %right.1), calls=%async_computation.1 | async-start | bytes 589824 | tf_op jit(solution)/shard_map/all_to_all | solution.py:213
  28.1 9.9 %collective-permute-start = (bf16[16,24,384]{2,1,0:T(8,128)(2,1)S(1)}, bf16[16,24,384]{2,1,0:T(8,128)(2,1)S(1)}, u32[]{:S(2)}, u32[]{:S(2)}) collective-permute-start(bf16[16,24,384]{2,1,0:T(8,128)(2,1)S(1)} %all-to-all-done), channel_id=1, source_target_pairs={{0,1},{1,0},{2,3},{3,2},{4,5},{5,4},{6,7},{7,6},{8,9},{9,8},{10,11... | collective-permute-start | bytes 884744 | tf_op jit(solution)/shard_map/ppermute | solution.py:215
  40.3 3.7 %copy-start.3 = (bf16[128,128]{1,0:T(8,128)(2,1)S(1)}, bf16[128,128]{1,0:T(8,128)(2,1)}, u32[]{:S(2)}) copy-start(bf16[128,128]{1,0:T(8,128)(2,1)} %w_ref.6) | copy-start | bytes 98308
  40.3 13.5 %all-to-all-start.2 = ((bf16[16,24,384]{2,1,0:T(8,128)(2,1)}), bf16[16,24,384]{2,1,0:T(8,128)(2,1)S(1)}, u32[]{:S(2)}, u32[]{:S(2)}) async-start(bf16[16,24,384]{2,1,0:T(8,128)(2,1)} %bitcast.6), calls=%async_computation.2 | async-start | bytes 589824 | tf_op jit(solution)/shard_map/all_to_all | solution.py:226
  44.0 9.9 %copy-start.4 = (bf16[128,128]{1,0:T(8,128)(2,1)S(1)}, bf16[128,128]{1,0:T(8,128)(2,1)}, u32[]{:S(2)}) copy-start(bf16[128,128]{1,0:T(8,128)(2,1)} %w_ref.7) | copy-start | bytes 98308
  53.8 0.7 %copy-start.5 = (f32[128]{0:T(128)S(1)}, f32[128]{0:T(128)}, u32[]{:S(2)}) copy-start(f32[128]{0:T(128)} %param.13) | copy-start | bytes 1540
  53.8 0.7 %copy-start.6 = (f32[128]{0:T(128)S(1)}, f32[128]{0:T(128)}, u32[]{:S(2)}) copy-start(f32[128]{0:T(128)} %param.14) | copy-start | bytes 1540

commit v3 on v2

v3 whole, which is shorter than its diff:
```python
import functools

import jax
import jax.numpy as jnp
from jax import lax
from jax.experimental import pallas as pl
from jax.experimental.pallas import tpu as pltpu
from jax.sharding import Mesh
from jax.sharding import PartitionSpec as P

LANES = 128
ROWS = 8
VMEM_LIMIT = 24 * 1024 * 1024
NT = (((1,), (1,)), ((), ()))


def layer_norm(values, scaling, offsets):
    average = jnp.mean(values, axis=-1, keepdims=True)
    centred = values - average
    variance = jnp.mean(centred * centred, axis=-1, keepdims=True)
    return centred * lax.rsqrt(variance + 1e-05) * scaling + offsets


def reorder_channels(values, row_count, other_count):
    shape_rest = values.shape[1:]
    grouped = values.reshape((row_count, other_count, -1) + shape_rest)
    return jnp.swapaxes(grouped, 0, 1).reshape(values.shape)


def plain_device(pair_input, in_gain, in_shift, w_proj, w_gate, out_gain, out_shift, w_out):
    row_count = lax.axis_size("row")
    others = ("col", "depth")
    other_count = lax.axis_size("col") * lax.axis_size("depth")
    channels = w_proj.shape[1] // 4
    normed = layer_norm(pair_input.astype(jnp.float32), in_gain, in_shift).astype(jnp.bfloat16)
    projected = jnp.einsum("xyc,cd->xyd", normed, w_proj, preferred_element_type=jnp.float32)
    sides = []
    for at in (0, 2 * channels):
        gate = jax.nn.sigmoid(projected[..., at : at + channels])
        side = (gate * projected[..., at + channels : at + 2 * channels]).astype(jnp.bfloat16)
        side = lax.all_to_all(side, "row", split_axis=2, concat_axis=0, tiled=True)
        sides.append(lax.all_to_all(side, others, split_axis=2, concat_axis=1, tiled=True))
    planes = jnp.einsum("kic,kjc->ijc", *sides, preferred_element_type=jnp.float32)
    product = lax.all_to_all(
        planes.astype(jnp.bfloat16), "row", split_axis=0, concat_axis=2, tiled=True
    )
    product = lax.all_to_all(product, others, split_axis=1, concat_axis=2, tiled=True)
    used = [reorder_channels(a, row_count, other_count) for a in (out_gain, out_shift, w_out)]
    product_norm = layer_norm(product.astype(jnp.float32), used[0], used[1]).astype(jnp.bfloat16)
    gating = jax.nn.sigmoid(
        jnp.einsum("xyc,cd->xyd", normed, w_gate, preferred_element_type=jnp.float32)
    )
    out = jnp.einsum("xyc,cd->xyd", product_norm, used[2], preferred_element_type=jnp.float32)
    return (gating * out).astype(jnp.bfloat16)


def spread(tiles):
    count = len(tiles)
    lane = lax.broadcasted_iota(jnp.int32, tiles[0].shape, 1)
    picked = [tiles[-v % count] for v in range(count)]
    step = 1
    while step < count:
        upper = (lane & step) != 0
        picked = [jnp.where(upper, picked[v - step], picked[v]) for v in range(count)]
        step *= 2
    return picked


def turn(tile, lanes):
    return pltpu.roll(tile, lanes % LANES, 1) if lanes % LANES else tile


def edges_kernel(
    split, x_hbm, gain_hbm, shift_hbm, w_hbm, wg_hbm, og_hbm, os_hbm, wo_hbm,
    out_ref, normed_ref, wg_ref, og_ref, os_ref, wo_ref, x_ref, gain_ref, shift_ref, w_ref, sems,
):
    rows, columns, channels = x_hbm.shape
    pairs = (
        (x_hbm, x_ref), (gain_hbm, gain_ref), (shift_hbm, shift_ref), (w_hbm, w_ref),
        (wg_hbm, wg_ref), (og_hbm, og_ref), (os_hbm, os_ref), (wo_hbm, wo_ref),
    )
    copies = [pltpu.make_async_copy(a, b, sems.at[n]) for n, (a, b) in enumerate(pairs)]
    for copy in copies:
        copy.start()
    for copy in copies[:4]:
        copy.wait()
    for k_group in range(rows // split):
        for i_tile in range(columns // ROWS):
            at = (slice(k_group * split, (k_group + 1) * split), slice(i_tile * ROWS, (i_tile + 1) * ROWS))
            values = x_ref[at].astype(jnp.float32).reshape(split * ROWS, channels)
            normed = layer_norm(values, gain_ref[...], shift_ref[...])
            normed_ref[at] = normed.reshape(split, ROWS, channels).astype(jnp.bfloat16)
            projected = jnp.dot(
                normed.astype(jnp.bfloat16), w_ref[...], preferred_element_type=jnp.float32
            )
            for side in range(2):
                gate = projected[:, 2 * side * channels : (2 * side + 1) * channels]
                value = projected[:, (2 * side + 1) * channels : (2 * side + 2) * channels]
                edge = jax.nn.sigmoid(gate) * value
                tiles = [turn(edge[k * ROWS : (k + 1) * ROWS], k) for k in range(split)]
                for s, tile in enumerate(spread(tiles)):
                    first = side * columns + i_tile * ROWS
                    out_ref[
                        s, first : first + ROWS, k_group * LANES : (k_group + 1) * LANES
                    ] = tile.astype(out_ref.dtype)
    for copy in copies[4:]:
        copy.wait()


def side_by_side(ref, at):
    return jnp.concatenate([ref[r, at, :] for r in range(ref.shape[0])], axis=1)


def group_masks(split, place, width):
    lane = lax.broadcasted_iota(jnp.int32, (split, LANES), 1)
    group = lax.shift_right_logical(
        (lane - place) & (LANES - 1), jnp.int32(split.bit_length() - 1)
    )
    return [
        jnp.concatenate([(group == g).astype(jnp.bfloat16)] * (width // LANES), axis=1)
        for g in range(LANES // split)
    ]


def slab_products(right, slab, masks):
    masked = jnp.concatenate([slab * mask for mask in masks], axis=0)
    return lax.dot_general(right, masked, NT, preferred_element_type=jnp.float32)


def pieces_of(split, columns, row_blocks):
    firsts = list(range(0, row_blocks * columns, ROWS))
    per = split // ROWS
    whole = len(firsts) // per * per
    order = [(core, first) for core in (0, 1) for first in firsts[:whole]]
    order += [(core, first) for core in (0, 1) for first in firsts[whole:]]
    return [order[n : n + per] for n in range(0, len(order), per)]


def own_kernel(split, place_ref, own_ref, right_ref, normed_ref, wg_ref, out_ref, gate_ref):
    row_count, rows, width = own_ref.shape
    columns = rows // row_count
    right = side_by_side(right_ref, slice(None))
    place = lax.shift_right_logical(place_ref[0], 1)
    masks = group_masks(split, place, row_count * width)
    for target in range(row_count):
        for slab in range(out_ref.shape[1]):
            first = target * columns + slab * split
            left = side_by_side(own_ref, slice(first, first + split))
            out_ref[target, slab] = slab_products(right, left, masks).astype(out_ref.dtype)
    rows, columns, channels = normed_ref.shape
    normed = normed_ref[...].reshape(rows * columns, channels)
    gate = jax.nn.sigmoid(jnp.dot(normed, wg_ref[...], preferred_element_type=jnp.float32))
    gate_ref[...] = gate.reshape(rows, columns, channels)


def other_kernel(split, slabs, place_ref, done_ref, own_ref, other_ref, right_ref, out_ref):
    row_count, rows, width = own_ref.shape
    columns = rows // row_count
    right = side_by_side(right_ref, slice(None))
    place = lax.shift_right_logical(place_ref[0], 1)
    masks = group_masks(split, place, row_count * width)
    refs = (own_ref, other_ref)
    for target in range(row_count):
        for n, slab in enumerate(slabs):
            lanes = slice(n * LANES, (n + 1) * LANES)
            if n < done_ref.shape[1]:
                out_ref[target, :, lanes] = done_ref[target, n]
                continue
            left = jnp.concatenate(
                [
                    side_by_side(refs[core], slice(target * columns + first, target * columns + first + ROWS))
                    for core, first in slab
                ],
                axis=0,
            )
            out_ref[target, :, lanes] = slab_products(right, left, masks).astype(out_ref.dtype)


def output_kernel(split, slabs, place_ref, sums_ref, gate_ref, gain_ref, shift_ref, w_ref, out_ref):
    columns = sums_ref.shape[1]
    channels = out_ref.shape[2]
    parity = place_ref[0] & 1
    for j_tile in range(columns // ROWS):
        js = slice(j_tile * ROWS, (j_tile + 1) * ROWS)
        for n, slab in enumerate(slabs):
            lanes = slice(n * LANES, (n + 1) * LANES)
            tiles = [turn(sums_ref[s, js, lanes].astype(jnp.float32), s) for s in range(split)]
            tiles = [turn(tile, -i) for i, tile in enumerate(spread(tiles))]
            values = jnp.concatenate(tiles, axis=0)
            normed = layer_norm(values, gain_ref[...], shift_ref[...]).astype(jnp.bfloat16)
            projected = jnp.dot(normed, w_ref[...], preferred_element_type=jnp.float32)
            for piece, (core, first) in enumerate(slab):
                block, inside = divmod(first, columns)
                core = parity if core == 0 else 1 - parity
                at = pl.ds((2 * block + core) * columns + inside, ROWS)
                value = projected[piece * ROWS * ROWS : (piece + 1) * ROWS * ROWS]
                value = value.reshape(ROWS, ROWS, channels)
                out_ref[at, js, :] = (gate_ref[at, js, :] * value).astype(out_ref.dtype)


SMEM = pl.BlockSpec(memory_space=pltpu.SMEM)
VMEM = pl.BlockSpec(memory_space=pltpu.VMEM)
HBM = pl.BlockSpec(memory_space=pltpu.HBM)


def call(kernel, name, out_shape, specs, flops, *arrays, scratch=()):
    outs = jax.tree.leaves(out_shape)
    moved = sum(a.size * a.dtype.itemsize for a in [*arrays, *outs])
    return pl.pallas_call(
        kernel,
        name=name,
        out_shape=out_shape,
        in_specs=specs,
        out_specs=jax.tree.map(lambda _: VMEM, out_shape),
        scratch_shapes=scratch,
        cost_estimate=pl.CostEstimate(flops=flops, bytes_accessed=moved, transcendentals=0),
        compiler_params=pltpu.CompilerParams(vmem_limit_bytes=VMEM_LIMIT),
    )(*arrays)


def fast_device(pair_input, in_gain, in_shift, w_proj, w_gate, out_gain, out_shift, w_out):
    rows, columns, channels = pair_input.shape
    row_count = lax.axis_size("row")
    owners = ("row", "col", "depth")
    split = row_count * lax.axis_size("col") * lax.axis_size("depth")
    width = rows // split * LANES
    per_row = split // row_count
    slabs = pieces_of(split, columns, rows // (2 * columns))
    own_slabs = sum(all(core == 0 for core, _ in slab) for slab in slabs)
    bf16, f32 = jnp.bfloat16, jnp.float32
    shape = jax.ShapeDtypeStruct
    gains = [a.reshape(1, channels) for a in (in_gain, in_shift, out_gain, out_shift)]
    flops = 4 * rows * columns * channels * channels
    place = lax.axis_index(("row", "col", "depth", "core")).astype(jnp.int32).reshape(1)

    edges, normed, wg, og, os, wo = call(
        functools.partial(edges_kernel, split),
        "edges",
        (
            shape((split, 2 * columns, width), bf16),
            shape(pair_input.shape, bf16),
            shape(w_gate.shape, bf16),
            shape((1, channels), f32),
            shape((1, channels), f32),
            shape(w_out.shape, bf16),
        ),
        [HBM] * 8,
        2 * flops,
        *(
            pltpu.with_memory_space_constraint(a, pltpu.HBM)
            for a in (pair_input, gains[0], gains[1], w_proj, w_gate, gains[2], gains[3], w_out)
        ),
        scratch=(
            pltpu.VMEM(pair_input.shape, bf16),
            pltpu.VMEM((1, channels), f32),
            pltpu.VMEM((1, channels), f32),
            pltpu.VMEM(w_proj.shape, bf16),
            pltpu.SemaphoreType.DMA((8,)),
        ),
    )
    exchange = functools.partial(
        lax.all_to_all, axis_name=owners, split_axis=0, concat_axis=0, tiled=True
    )
    edges = exchange(edges)
    own, right = edges[:, :columns], edges[:, columns:]
    other = lax.ppermute(own, "core", [(0, 1), (1, 0)])
    stacked = (row_count, per_row * columns, width)
    own, other, right = (a.reshape(stacked) for a in (own, other, right))
    done, gate = call(
        functools.partial(own_kernel, split),
        "own",
        (
            shape((row_count, own_slabs, per_row * columns, LANES), bf16),
            shape(pair_input.shape, f32),
        ),
        [SMEM] + [VMEM] * 4,
        flops,
        place, own, right, normed, wg,
    )
    sums = call(
        functools.partial(other_kernel, split, slabs),
        "other",
        shape(stacked, bf16),
        [SMEM] + [VMEM] * 4,
        flops,
        place, done, own, other, right,
    )
    sums = exchange(sums.reshape(split, columns, width))
    return call(
        functools.partial(output_kernel, split, slabs),
        "output",
        shape(pair_input.shape, bf16),
        [SMEM] + [VMEM] * 5,
        flops // 2,
        place, sums, gate, og, os, wo,
    )


def suits(mesh, pair_input, w_proj):
    row_count, col_count, depth_count = (mesh.shape[a] for a in ("row", "col", "depth"))
    split = row_count * col_count * depth_count // 2
    rows, columns = pair_input.shape[0] // row_count, pair_input.shape[1] // (col_count * depth_count)
    return (
        depth_count % 2 == 0
        and pair_input.shape[0] == pair_input.shape[1]
        and pair_input.shape[2] == LANES
        and w_proj.shape == (LANES, 4 * LANES)
        and split & (split - 1) == 0
        and split >= 16
        and LANES % split == 0
        and rows % split == 0
        and columns % ROWS == 0
        and rows % (2 * columns) == 0
    )


def solution(mesh):
    def step(pair_input, in_gain, in_shift, w_proj, w_gate, out_gain, out_shift, w_out):
        if suits(mesh, pair_input, w_proj):
            row_count, col_count, depth_count = mesh.devices.shape
            used = Mesh(
                mesh.devices.reshape(row_count, col_count, depth_count // 2, 2),
                ("row", "col", "depth", "core"),
            )
            pair, body = P("row", ("col", "depth", "core"), None), fast_device
        else:
            used, pair, body = mesh, P("row", ("col", "depth"), None), plain_device
        return jax.shard_map(
            body,
            mesh=used,
            in_specs=(pair, P(), P(), P(), P(), P(), P(), P()),
            out_specs=pair,
            check_vma=False,
        )(pair_input, in_gain, in_shift, w_proj, w_gate, out_gain, out_shift, w_out)

    return step
```

time: 57.5 us -> 47 us (0.82)
  blocking collectives: 0 us -> 39.5 us
  waiting for transfers between devices: 28.8 us -> 0.83 us
  starting transfers between devices: 15.8 us -> 0.07 us
  local copies, waits for them, and re-layouts: 3.22 us -> 0.06 us
  Pallas kernels: 9.2 us -> 6.37 us
    all_to_all x0 -> x2, blocking collectives: none -> 39.5 us  [the longest x1 25.6 us: fast_device(): edges = exchange(edges)]
    all_to_all x3 -> x0, waiting for transfers between devices: 28.8 us -> none  [the longest x1 9.86 us: fast_device(): exchange(call(functools.partial(right_kernel, split), 'right', message, f...]
    all_to_all x3 -> x0, starting transfers between devices: 15.7 us -> none  [the longest x1 8.47 us: fast_device(): own = exchange(left)]
    unnamed x18 -> x0, local copies, waits for them, and re-layouts: 3.22 us -> none
    pallas_call x5 -> x4, Pallas kernels: 9.2 us -> 6.37 us  [call(): pl.pallas_call(kernel, name=name, out_shape=out_shape, in_specs=specs, ou...]
    ppermute x1, waiting for transfers between devices: 0.01 us -> 0.83 us  [fast_device(): other = lax.ppermute(own, 'core', [(0, 1), (1, 0)])]
  transfers between devices with their start and end apart: 4 -> 1, of which waited for: 3 -> 1; matrix products, arithmetic and copies ran while one was open for 0% -> 0% of each run, Pallas kernels for 3% -> 2%
where the time goes in v3:
time: 47 us; the launch traced here: 46.8 us
  blocking collectives  39.5 us (84%)
  Pallas kernels  6.37 us (14%)
  waiting for transfers between devices  0.83 us (2%)
    all_to_all x1, blocking collectives, fast_device(): edges = exchange(edges)  25.6 us
    all_to_all x1, blocking collectives, fast_device(): sums = exchange(sums.reshape(split, columns, width))  13.9 us
    pallas_call x4, Pallas kernels, call(): pl.pallas_call(kernel, name=name, out_shape=out_shape, in_specs=specs, ou...  6.37 us
  transfers between devices with their start and end apart: 1, of which 1 were waited for; matrix products, arithmetic and copies ran while one was open for 0% of the time, Pallas kernels for 2%

profile of v3, /device:TPU:0, one launch (start us, length us, event | category | flops | bytes accessed | tf_op | source)
XLA Modules:
  0.0 46.8 jit_solution(9297827781723996750)
XLA Ops:
  0.0 2.6 %edges.1 = (bf16[16,48,384]{2,1,0:T(8,128)(2,1)S(1)}, bf16[48,24,128]{2,1,0:T(8,128)(2,1)S(1)}, bf16[128,128]{1,0:T(8,128)(2,1)S(1)}, f32[1,128]{1,0:T(1,128)S(1...) custom-call(bf16[48,24,128]{2,1,0:T(8,128)(2,1)} %x_hbm.1, f32[1,128]{1,0:T(1,128)} %bitcast.15, ...), custom_call_target="tpu_custom_call" | custom-call | flops 150994944 | bytes 1444864 | tf_op jit(solution)/shard_map/edges/pallas_call | solution.py:209
  2.6 25.6 %all_to_all.10 = bf16[16,48,384]{2,1,0:T(8,128)(2,1)S(1)} all-to-all(bf16[16,48,384]{2,1,0:T(8,128)(2,1)S(1)} %get-tuple-element.13), channel_id=1, replica_groups=mesh['row'=4,'col'=2,'depth'=2,'core'=2] {'row','col','depth'}, dimensions={0} | all-to-all | bytes 1179648 | tf_op jit(solution)/shard_map/all_to_all | solution.py:264
  28.2 0.1 fusion
  28.3 0.1 collective-permute-start
  28.4 0.7 %own.1 = (bf16[4,1,96,128]{3,2,1,0:T(8,128)(2,1)S(1)}, f32[48,24,128]{2,1,0:T(8,128)S(1)}) custom-call(s32[1]{0:T(128)} %bitcast.place_ref, bf16[4,96,384]{2,1,0:T(8,128)(2,1)S(1)} %bitcast.11, bf16[4,96,384]{2,1,0:T(8,128)(2,1)S(1)} %bitcast.9, bf16[48,24,128]{2,1,0:T(8,128)(2,1)S(1)} %get-tuple-element.14.normed_ref, ...), custom_call_target="tpu_custom_call" | custom-call | flops 75497472 | bytes 1605636 | tf_op jit(solution)/shard_map/own/pallas_call | solution.py:209
  29.1 0.8 %collective-permute-done = bf16[16,24,384]{2,1,0:T(8,128)(2,1)S(1)} collective-permute-done((bf16[16,24,384]{2,1,0:T(8,128)(2,1)S(1)}, bf16[16,24,384]{2,1,0:T(8,128)(2,1)S(1)}, u32[]{:S(2)}, u32[]{:S(2)}) %collective-permute-start) | collective-permute-done | bytes 294944 | tf_op jit(solution)/shard_map/ppermute | solution.py:266
  29.9 1.1 %other.1 = bf16[4,96,384]{2,1,0:T(8,128)(2,1)S(1)} custom-call(s32[1]{0:T(128)} %bitcast.place_ref, bf16[4,1,96,128]{3,2,1,0:T(8,128)(2,1)S(1)} %get-tuple-element.16.done_ref, bf16[4,96,384]{2,1,0:T(8,128)(2,1)S(1)} %bitcast.12, bf16[4,96,384]{2,1,0:T(8,128)(2,1)S(1)} %bitcast.14, bf16[4,96,384]{2,1,0:T(8,128)(2,1)S(1)} %bitcast.10), custom_call_target="tpu_custom_call" | custom-call | flops 75497472 | bytes 1277956 | tf_op jit(solution)/shard_map/other/pallas_call | solution.py:209
  31.0 13.9 %all_to_all.11.sums_ref = bf16[16,24,384]{2,1,0:T(8,128)(2,1)S(1)} all-to-all(bf16[16,24,384]{2,1,0:T(8,128)(2,1)S(1)} %bitcast.13), channel_id=1, replica_groups=mesh['row'=4,'col'=2,'depth'=2,'core'=2] {'row','col','depth'}, dimensions={0} | all-to-all | bytes 589824 | tf_op jit(solution)/shard_map/all_to_all | solution.py:288
  44.9 1.9 %output.1 = bf16[48,24,128]{2,1,0:T(8,128)(2,1)} custom-call(s32[1]{0:T(128)} %bitcast.place_ref, bf16[16,24,384]{2,1,0:T(8,128)(2,1)S(1)} %all_to_all.11.sums_ref, f32[48,24,128]{2,1,0:T(8,128)S(1)} %get-tuple-element.17.gate_ref, f32[1,128]{1,0:T(1,128)S(1)} %get-tuple-element.18.gain_ref, f32[1,128]{1,0:T(1,128)S(1)} %get-tuple-element.19.shift_ref, ...), custom_call_target="tpu_custom_call" | custom-call | flops 37748736 | bytes 1213444 | tf_op jit(solution)/shard_map/output/pallas_call | solution.py:209
Async XLA Ops:
  28.3 1.6 %collective-permute-start = (bf16[16,24,384]{2,1,0:T(8,128)(2,1)S(1)}, bf16[16,24,384]{2,1,0:T(8,128)(2,1)S(1)}, u32[]{:S(2)}, u32[]{:S(2)}) collective-permute-start(bf16[16,24,384]{2,1,0:T(8,128)(2,1)S(1)} %get-tuple-element.22), channel_id=1, source_target_pairs={{0,1},{1,0},{2,3},{3,2},{4,5},{5,4},{6,7},{7,6},{8,9},{9,8},{10,11... | collective-permute-start | bytes 884744 | tf_op jit(solution)/shard_map/ppermute | solution.py:266

commit v4 on v3

--- a/solution.py
+++ b/solution.py
@@ -70,6 +70,13 @@
     return pltpu.roll(tile, lanes % LANES, 1) if lanes % LANES else tile
 
 
+def kernel_norm(values, scaling, offsets):
+    share = jnp.full((LANES, LANES), 1 / LANES, jnp.bfloat16)
+    centred = values.astype(jnp.float32) - jnp.dot(values, share, preferred_element_type=jnp.float32)
+    variance = jnp.mean(centred * centred, axis=-1, keepdims=True)
+    return (centred * lax.rsqrt(variance + 1e-05) * scaling + offsets).astype(jnp.bfloat16)
+
+
 def edges_kernel(
     split, x_hbm, gain_hbm, shift_hbm, w_hbm, wg_hbm, og_hbm, os_hbm, wo_hbm,
     out_ref, normed_ref, wg_ref, og_ref, os_ref, wo_ref, x_ref, gain_ref, shift_ref, w_ref, sems,
@@ -84,47 +91,85 @@
         copy.start()
     for copy in copies[:4]:
         copy.wait()
-    for k_group in range(rows // split):
+    normed = []
+    for slab in range(rows // split):
+        ks = slice(slab * split, (slab + 1) * split)
+        values = x_ref[ks].reshape(split * columns, channels)
+        normed.append(kernel_norm(values, gain_ref[...], shift_ref[...]))
+        normed_ref[ks] = normed[-1].reshape(split, columns, channels)
+    for slab, values in enumerate(normed):
+        projected = jnp.dot(values, w_ref[...], preferred_element_type=jnp.float32)
         for i_tile in range(columns // ROWS):
-            at = (slice(k_group * split, (k_group + 1) * split), slice(i_tile * ROWS, (i_tile + 1) * ROWS))
-            values = x_ref[at].astype(jnp.float32).reshape(split * ROWS, channels)
-            normed = layer_norm(values, gain_ref[...], shift_ref[...])
-            normed_ref[at] = normed.reshape(split, ROWS, channels).astype(jnp.bfloat16)
-            projected = jnp.dot(
-                normed.astype(jnp.bfloat16), w_ref[...], preferred_element_type=jnp.float32
-            )
-            for side in range(2):
-                gate = projected[:, 2 * side * channels : (2 * side + 1) * channels]
-                value = projected[:, (2 * side + 1) * channels : (2 * side + 2) * channels]
-                edge = jax.nn.sigmoid(gate) * value
-                tiles = [turn(edge[k * ROWS : (k + 1) * ROWS], k) for k in range(split)]
-                for s, tile in enumerate(spread(tiles)):
-                    first = side * columns + i_tile * ROWS
-                    out_ref[
-                        s, first : first + ROWS, k_group * LANES : (k_group + 1) * LANES
-                    ] = tile.astype(out_ref.dtype)
+            tiles = []
+            for k in range(split):
+                first = k * columns + i_tile * ROWS
+                part = projected[first : first + ROWS]
+                parts = [part[:, n * channels : (n + 1) * channels] for n in range(4)]
+                left = jax.nn.sigmoid(parts[0]) * parts[1]
+                right = jax.nn.sigmoid(parts[2]) * parts[3]
+                both = jnp.concatenate([left, right], axis=0).astype(out_ref.dtype)
+                tiles.append(turn(both, k))
+            for s, tile in enumerate(spread(tiles)):
+                at = slice(2 * i_tile * ROWS, 2 * (i_tile + 1) * ROWS)
+                out_ref[s, at, slab * LANES : (slab + 1) * LANES] = tile
     for copy in copies[4:]:
         copy.wait()
 
 
-def side_by_side(ref, at):
-    return jnp.concatenate([ref[r, at, :] for r in range(ref.shape[0])], axis=1)
-
-
-def group_masks(split, place, width):
-    lane = lax.broadcasted_iota(jnp.int32, (split, LANES), 1)
-    group = lax.shift_right_logical(
-        (lane - place) & (LANES - 1), jnp.int32(split.bit_length() - 1)
-    )
+def place_in(*axes):
+    place = lax.axis_index(axes[0])
+    for axis in axes[1:]:
+        place = place * lax.axis_size(axis) + lax.axis_index(axis)
+    return place
+
+
+def lane_place(shape, place):
+    return (lax.broadcasted_iota(jnp.int32, shape, 1) - place) & (LANES - 1)
+
+
+def k_tiles(ref, at):
     return [
-        jnp.concatenate([(group == g).astype(jnp.bfloat16)] * (width // LANES), axis=1)
-        for g in range(LANES // split)
+        ref[r, at, t * LANES : (t + 1) * LANES]
+        for r in range(ref.shape[0])
+        for t in range(ref.shape[2] // LANES)
     ]
 
 
-def slab_products(right, slab, masks):
-    masked = jnp.concatenate([slab * mask for mask in masks], axis=0)
-    return lax.dot_general(right, masked, NT, preferred_element_type=jnp.float32)
+def fold(tiles, place):
+    low = lane_place(tiles[0].shape, place) < LANES // 2
+    halves = ([], [])
+    for first, second in zip(tiles[::2], tiles[1::2]):
+        halves[0].append(jnp.where(low, first, turn(second, LANES // 2)))
+        halves[1].append(jnp.where(low, turn(first, LANES // 2), second))
+    return [jnp.concatenate(half, axis=1) for half in halves]
+
+
+def slab_products(split, place, rights, units):
+    groups = LANES // split // 2
+    shift = split.bit_length() - 1
+    position = lane_place((split, LANES), place)
+    group = lax.shift_right_logical(position, jnp.int32(shift)) & (groups - 1)
+    count = rights[0].shape[1] // LANES
+    masks = [
+        jnp.concatenate([(group == g).astype(jnp.bfloat16)] * count, axis=1) for g in range(groups)
+    ]
+    masked = ([], [])
+    for unit in units:
+        for half, folded in enumerate(fold(unit, place)):
+            masked[half].extend(folded * mask for mask in masks)
+    low, high = (
+        lax.dot_general(
+            right, jnp.concatenate(parts, axis=0), NT, preferred_element_type=jnp.float32
+        ).astype(jnp.bfloat16)
+        for right, parts in zip(rights, masked)
+    )
+    first_half = lax.broadcasted_iota(jnp.int32, (rights[0].shape[0], LANES), 1) < LANES // 2
+    out = []
+    for n in range(0, len(units) * LANES // 2, LANES):
+        lows, highs = low[:, n : n + LANES], high[:, n : n + LANES]
+        out.append(jnp.where(first_half, lows, turn(highs, LANES // 2)))
+        out.append(jnp.where(first_half, turn(lows, LANES // 2), highs))
+    return out
 
 
 def pieces_of(split, columns, row_blocks):
@@ -136,69 +181,79 @@
     return [order[n : n + per] for n in range(0, len(order), per)]
 
 
-def own_kernel(split, place_ref, own_ref, right_ref, normed_ref, wg_ref, out_ref, gate_ref):
-    row_count, rows, width = own_ref.shape
+def own_kernel(split, own_ref, right_ref, normed_ref, wg_ref, out_ref, gate_ref, rights_ref):
+    row_count, rows, _ = own_ref.shape
     columns = rows // row_count
-    right = side_by_side(right_ref, slice(None))
-    place = lax.shift_right_logical(place_ref[0], 1)
-    masks = group_masks(split, place, row_count * width)
-    for target in range(row_count):
-        for slab in range(out_ref.shape[1]):
-            first = target * columns + slab * split
-            left = side_by_side(own_ref, slice(first, first + split))
-            out_ref[target, slab] = slab_products(right, left, masks).astype(out_ref.dtype)
+    place = place_in("row", "col", "depth")
+    rights = fold(k_tiles(right_ref, slice(None)), place)
+    for half in range(2):
+        rights_ref[half] = rights[half]
+    slots = [(target, slab) for target in range(row_count) for slab in range(out_ref.shape[1])]
+    units = []
+    for target, slab in slots:
+        first = target * columns + slab * split
+        units.append(k_tiles(own_ref, slice(first, first + split)))
+    for (target, slab), block in zip(slots, slab_products(split, place, rights, units)):
+        out_ref[target, slab] = block
     rows, columns, channels = normed_ref.shape
     normed = normed_ref[...].reshape(rows * columns, channels)
     gate = jax.nn.sigmoid(jnp.dot(normed, wg_ref[...], preferred_element_type=jnp.float32))
     gate_ref[...] = gate.reshape(rows, columns, channels)
 
 
-def other_kernel(split, slabs, place_ref, done_ref, own_ref, other_ref, right_ref, out_ref):
-    row_count, rows, width = own_ref.shape
+def other_kernel(split, slabs, done_ref, own_ref, other_ref, rights_ref, out_ref):
+    row_count, rows, _ = own_ref.shape
     columns = rows // row_count
-    right = side_by_side(right_ref, slice(None))
-    place = lax.shift_right_logical(place_ref[0], 1)
-    masks = group_masks(split, place, row_count * width)
+    place = place_in("row", "col", "depth")
+    rights = [rights_ref[half] for half in range(2)]
     refs = (own_ref, other_ref)
-    for target in range(row_count):
-        for n, slab in enumerate(slabs):
-            lanes = slice(n * LANES, (n + 1) * LANES)
-            if n < done_ref.shape[1]:
-                out_ref[target, :, lanes] = done_ref[target, n]
-                continue
-            left = jnp.concatenate(
-                [
-                    side_by_side(refs[core], slice(target * columns + first, target * columns + first + ROWS))
-                    for core, first in slab
-                ],
-                axis=0,
-            )
-            out_ref[target, :, lanes] = slab_products(right, left, masks).astype(out_ref.dtype)
-
-
-def output_kernel(split, slabs, place_ref, sums_ref, gate_ref, gain_ref, shift_ref, w_ref, out_ref):
+    done = done_ref.shape[1]
+    for start in range(0, row_count, 2):
+        slots, units = [], []
+        for target in (start, start + 1):
+            for slab in range(done):
+                out_ref[target, :, slab * LANES : (slab + 1) * LANES] = done_ref[target, slab]
+            for slab in range(done, len(slabs)):
+                pieces = [
+                    k_tiles(refs[core], slice(target * columns + first, target * columns + first + ROWS))
+                    for core, first in slabs[slab]
+                ]
+                slots.append((target, slab))
+                units.append([jnp.concatenate(parts, axis=0) for parts in zip(*pieces)])
+        for (target, slab), block in zip(slots, slab_products(split, place, rights, units)):
+            out_ref[target, :, slab * LANES : (slab + 1) * LANES] = block
+
+
+def output_kernel(split, slabs, sums_ref, gate_ref, gain_ref, shift_ref, w_ref, out_ref):
     columns = sums_ref.shape[1]
     channels = out_ref.shape[2]
-    parity = place_ref[0] & 1
-    for j_tile in range(columns // ROWS):
-        js = slice(j_tile * ROWS, (j_tile + 1) * ROWS)
-        for n, slab in enumerate(slabs):
-            lanes = slice(n * LANES, (n + 1) * LANES)
-            tiles = [turn(sums_ref[s, js, lanes].astype(jnp.float32), s) for s in range(split)]
-            tiles = [turn(tile, -i) for i, tile in enumerate(spread(tiles))]
-            values = jnp.concatenate(tiles, axis=0)
-            normed = layer_norm(values, gain_ref[...], shift_ref[...]).astype(jnp.bfloat16)
-            projected = jnp.dot(normed, w_ref[...], preferred_element_type=jnp.float32)
-            for piece, (core, first) in enumerate(slab):
-                block, inside = divmod(first, columns)
-                core = parity if core == 0 else 1 - parity
-                at = pl.ds((2 * block + core) * columns + inside, ROWS)
-                value = projected[piece * ROWS * ROWS : (piece + 1) * ROWS * ROWS]
-                value = value.reshape(ROWS, ROWS, channels)
-                out_ref[at, js, :] = (gate_ref[at, js, :] * value).astype(out_ref.dtype)
-
-
-SMEM = pl.BlockSpec(memory_space=pltpu.SMEM)
+    parity = lax.axis_index("core")
+
+    def finish(tiles, n, js):
+        normed = kernel_norm(jnp.concatenate(tiles, axis=0), gain_ref[...], shift_ref[...])
+        projected = jnp.dot(normed, w_ref[...], preferred_element_type=jnp.float32)
+        for piece, (core, first) in enumerate(slabs[n]):
+            block, inside = divmod(first, columns)
+            core = parity if core == 0 else 1 - parity
+            at = pl.ds((2 * block + core) * columns + inside, ROWS)
+            value = projected[piece * ROWS * ROWS : (piece + 1) * ROWS * ROWS]
+            value = value.reshape(ROWS, ROWS, channels)
+            out_ref[at, js, :] = (gate_ref[at, js, :] * value).astype(out_ref.dtype)
+
+    units = [
+        (n, slice(first, first + ROWS)) for n in range(len(slabs)) for first in range(0, columns, ROWS)
+    ]
+    for start in range(0, len(units), 2):
+        both = units[start : start + 2]
+        tiles = []
+        for s in range(split):
+            parts = [sums_ref[s, js, n * LANES : (n + 1) * LANES] for n, js in both]
+            tiles.append(turn(jnp.concatenate(parts, axis=0), s))
+        tiles = [turn(tile, -i) for i, tile in enumerate(spread(tiles))]
+        for at, (n, js) in enumerate(both):
+            finish([tile[at * ROWS : (at + 1) * ROWS] for tile in tiles], n, js)
+
+
 VMEM = pl.BlockSpec(memory_space=pltpu.VMEM)
 HBM = pl.BlockSpec(memory_space=pltpu.HBM)
 
@@ -231,7 +286,6 @@
     shape = jax.ShapeDtypeStruct
     gains = [a.reshape(1, channels) for a in (in_gain, in_shift, out_gain, out_shift)]
     flops = 4 * rows * columns * channels * channels
-    place = lax.axis_index(("row", "col", "depth", "core")).astype(jnp.int32).reshape(1)
 
     edges, normed, wg, og, os, wo = call(
         functools.partial(edges_kernel, split),
@@ -262,37 +316,39 @@
         lax.all_to_all, axis_name=owners, split_axis=0, concat_axis=0, tiled=True
     )
     edges = exchange(edges)
-    own, right = edges[:, :columns], edges[:, columns:]
+    edges = edges.reshape(split, columns // ROWS, 2, ROWS, width)
+    own, right = (edges[:, :, side].reshape(split, columns, width) for side in range(2))
     other = lax.ppermute(own, "core", [(0, 1), (1, 0)])
     stacked = (row_count, per_row * columns, width)
     own, other, right = (a.reshape(stacked) for a in (own, other, right))
-    done, gate = call(
+    done, gate, rights = call(
         functools.partial(own_kernel, split),
         "own",
         (
             shape((row_count, own_slabs, per_row * columns, LANES), bf16),
             shape(pair_input.shape, f32),
+            shape((2, per_row * columns, row_count * width // 2), bf16),
         ),
-        [SMEM] + [VMEM] * 4,
+        [VMEM] * 4,
         flops,
-        place, own, right, normed, wg,
+        own, right, normed, wg,
     )
     sums = call(
         functools.partial(other_kernel, split, slabs),
         "other",
         shape(stacked, bf16),
-        [SMEM] + [VMEM] * 4,
+        [VMEM] * 4,
         flops,
-        place, done, own, other, right,
+        done, own, other, rights,
     )
     sums = exchange(sums.reshape(split, columns, width))
     return call(
         functools.partial(output_kernel, split, slabs),
         "output",
         shape(pair_input.shape, bf16),
-        [SMEM] + [VMEM] * 5,
+        [VMEM] * 5,
         flops // 2,
-        place, sums, gate, og, os, wo,
+        sums, gate, og, os, wo,
     )
 
 
@@ -307,7 +363,8 @@
         and w_proj.shape == (LANES, 4 * LANES)
         and split & (split - 1) == 0
         and split >= 16
-        and LANES % split == 0
+        and LANES % (2 * split) == 0
+        and row_count % 2 == 0
         and rows % split == 0
         and columns % ROWS == 0
         and rows % (2 * columns) == 0

time: 47 us -> 45.5 us (0.968)
  Pallas kernels: 6.37 us -> 4.67 us
    pallas_call x4, Pallas kernels: 6.37 us -> 4.67 us  [call(): pl.pallas_call(kernel, name=name, out_shape=out_shape, in_specs=specs, ou...]
  transfers between devices with their start and end apart: 1 -> 1, of which waited for: 1 -> 1; matrix products, arithmetic and copies ran while one was open for 0% -> 0% of each run, Pallas kernels for 2% -> 1%
where the time goes in v4:
time: 45.5 us; the launch traced here: 45.3 us
  blocking collectives  39.4 us (87%)
  Pallas kernels  4.67 us (10%)
  waiting for transfers between devices  1.01 us (2%)
    all_to_all x1, blocking collectives, fast_device(): edges = exchange(edges)  25.6 us
    all_to_all x1, blocking collectives, fast_device(): sums = exchange(sums.reshape(split, columns, width))  13.8 us
    pallas_call x4, Pallas kernels, call(): pl.pallas_call(kernel, name=name, out_shape=out_shape, in_specs=specs, ou...  4.67 us
    ppermute x1, waiting for transfers between devices, fast_device(): other = lax.ppermute(own, 'core', [(0, 1), (1, 0)])  1.01 us
  transfers between devices with their start and end apart: 1, of which 1 were waited for; matrix products, arithmetic and copies ran while one was open for 0% of the time, Pallas kernels for 1%

profile of v4, /device:TPU:0, one launch (start us, length us, event | category | flops | bytes accessed | tf_op | source)
XLA Modules:
  0.0 45.3 jit_solution(8035492117540143568)
XLA Ops:
  0.0 1.9 %edges.1 = (bf16[16,48,384]{2,1,0:T(8,128)(2,1)S(1)}, bf16[48,24,128]{2,1,0:T(8,128)(2,1)S(1)}, bf16[128,128]{1,0:T(8,128)(2,1)S(1)}, f32[1,128]{1,0:T(1,128)S(1...) custom-call(bf16[48,24,128]{2,1,0:T(8,128)(2,1)} %x_hbm.1, f32[1,128]{1,0:T(1,128)} %bitcast.22, ...), custom_call_target="tpu_custom_call" | custom-call | flops 150994944 | bytes 1444864 | tf_op jit(solution)/shard_map/edges/pallas_call | solution.py:264
  1.9 25.6 %all_to_all.10 = bf16[16,48,384]{2,1,0:T(8,128)(2,1)S(1)} all-to-all(bf16[16,48,384]{2,1,0:T(8,128)(2,1)S(1)} %get-tuple-element.14), channel_id=1, replica_groups=mesh['row'=4,'col'=2,'depth'=2,'core'=2] {'row','col','depth'}, dimensions={0} | all-to-all | bytes 1179648 | tf_op jit(solution)/shard_map/all_to_all | solution.py:318
  27.5 0.1 slice_bitcast_fusion
  27.6 0.1 collective-permute-start
  27.7 0.6 %own.1 = (bf16[4,1,96,128]{3,2,1,0:T(8,128)(2,1)S(1)}, f32[48,24,128]{2,1,0:T(8,128)S(1)}, bf16[2,96,768]{2,1,0:T(8,128)(2,1)S(1)}) custom-call(bf16[4,96,384]{2,1,0:T(8,128)(2,1)S(1)} %bitcast.16, bf16[4,96,384]{2,1,0:T(8,128)(2,1)S(1)} %bitcast.19, bf16[48,24,128]{2,1,0:T(8,128)(2,1)S(1)} %get-tuple-element.15.normed_ref, ...), custom_call_target="tpu_custom_call" | custom-call | flops 75497472 | bytes 1900544 | tf_op jit(solution)/shard_map/own/pallas_call | solution.py:264
  28.3 1.0 %collective-permute-done = bf16[16,24,384]{2,1,0:T(8,128)(2,1)S(1)} collective-permute-done((bf16[16,24,384]{2,1,0:T(8,128)(2,1)S(1)}, bf16[16,24,384]{2,1,0:T(8,128)(2,1)S(1)}, u32[]{:S(2)}, u32[]{:S(2)}) %collective-permute-start) | collective-permute-done | bytes 294944 | tf_op jit(solution)/shard_map/ppermute | solution.py:321
  29.3 0.8 %other.1 = bf16[4,96,384]{2,1,0:T(8,128)(2,1)S(1)} custom-call(bf16[4,1,96,128]{3,2,1,0:T(8,128)(2,1)S(1)} %get-tuple-element.17.done_ref, bf16[4,96,384]{2,1,0:T(8,128)(2,1)S(1)} %bitcast.17, bf16[4,96,384]{2,1,0:T(8,128)(2,1)S(1)} %bitcast.20, bf16[2,96,768]{2,1,0:T(8,128)(2,1)S(1)} %get-tuple-element.18.rights_ref), custom_call_target="tpu_custom_call" | custom-call | flops 75497472 | bytes 1277952 | tf_op jit(solution)/shard_map/other/pallas_call | solution.py:264
  30.0 13.8 %all_to_all.11.sums_ref = bf16[16,24,384]{2,1,0:T(8,128)(2,1)S(1)} all-to-all(bf16[16,24,384]{2,1,0:T(8,128)(2,1)S(1)} %bitcast.18), channel_id=1, replica_groups=mesh['row'=4,'col'=2,'depth'=2,'core'=2] {'row','col','depth'}, dimensions={0} | all-to-all | bytes 589824 | tf_op jit(solution)/shard_map/all_to_all | solution.py:344
  43.9 1.4 %output.1 = bf16[48,24,128]{2,1,0:T(8,128)(2,1)} custom-call(bf16[16,24,384]{2,1,0:T(8,128)(2,1)S(1)} %all_to_all.11.sums_ref, f32[48,24,128]{2,1,0:T(8,128)S(1)} %get-tuple-element.19.gate_ref, f32[1,128]{1,0:T(1,128)S(1)} %get-tuple-element.20.gain_ref, f32[1,128]{1,0:T(1,128)S(1)} %get-tuple-element.21.shift_ref, bf16[128,128]{1,0:T(8,128)(2,1)S(1)} %get-tuple-element.22.w_ref), custom_call_target="tpu_custom_call" | custom-call | flops 37748736 | bytes 1213440 | tf_op jit(solution)/shard_map/output/pallas_call | solution.py:264
Async XLA Ops:
  27.6 1.6 %collective-permute-start = (bf16[16,24,384]{2,1,0:T(8,128)(2,1)S(1)}, bf16[16,24,384]{2,1,0:T(8,128)(2,1)S(1)}, u32[]{:S(2)}, u32[]{:S(2)}) collective-permute-start(bf16[16,24,384]{2,1,0:T(8,128)(2,1)S(1)} %get-tuple-element.23), channel_id=1, source_target_pairs={{0,1},{1,0},{2,3},{3,2},{4,5},{5,4},{6,7},{7,6},{8,9},{9,8},{10,11... | collective-permute-start | bytes 884744 | tf_op jit(solution)/shard_map/ppermute | solution.py:321

commit v5 on v4

--- a/solution.py
+++ b/solution.py
@@ -81,6 +81,7 @@
     split, x_hbm, gain_hbm, shift_hbm, w_hbm, wg_hbm, og_hbm, os_hbm, wo_hbm,
     out_ref, normed_ref, wg_ref, og_ref, os_ref, wo_ref, x_ref, gain_ref, shift_ref, w_ref, sems,
 ):
+    core = lax.axis_index("core")
     rows, columns, channels = x_hbm.shape
     pairs = (
         (x_hbm, x_ref), (gain_hbm, gain_ref), (shift_hbm, shift_ref), (w_hbm, w_ref),
@@ -110,8 +111,10 @@
                 both = jnp.concatenate([left, right], axis=0).astype(out_ref.dtype)
                 tiles.append(turn(both, k))
             for s, tile in enumerate(spread(tiles)):
-                at = slice(2 * i_tile * ROWS, 2 * (i_tile + 1) * ROWS)
-                out_ref[s, at, slab * LANES : (slab + 1) * LANES] = tile
+                at = slice(i_tile * ROWS, (i_tile + 1) * ROWS)
+                lanes = slice(slab * LANES, (slab + 1) * LANES)
+                out_ref[s, 1 - core, at, lanes] = tile[:ROWS]
+                out_ref[s, core, at, lanes] = tile[ROWS:]
     for copy in copies[4:]:
         copy.wait()
 
@@ -227,7 +230,7 @@
 def output_kernel(split, slabs, sums_ref, gate_ref, gain_ref, shift_ref, w_ref, out_ref):
     columns = sums_ref.shape[1]
     channels = out_ref.shape[2]
-    parity = lax.axis_index("core")
+    parity = 1 - lax.axis_index("core")
 
     def finish(tiles, n, js):
         normed = kernel_norm(jnp.concatenate(tiles, axis=0), gain_ref[...], shift_ref[...])
@@ -291,7 +294,7 @@
         functools.partial(edges_kernel, split),
         "edges",
         (
-            shape((split, 2 * columns, width), bf16),
+            shape((split, 2, columns, width), bf16),
             shape(pair_input.shape, bf16),
             shape(w_gate.shape, bf16),
             shape((1, channels), f32),
@@ -312,12 +315,15 @@
             pltpu.SemaphoreType.DMA((8,)),
         ),
     )
-    exchange = functools.partial(
-        lax.all_to_all, axis_name=owners, split_axis=0, concat_axis=0, tiled=True
-    )
-    edges = exchange(edges)
-    edges = edges.reshape(split, columns // ROWS, 2, ROWS, width)
-    own, right = (edges[:, :, side].reshape(split, columns, width) for side in range(2))
+    exchange = functools.partial(lax.all_to_all, split_axis=0, concat_axis=0, tiled=True)
+    core = lax.axis_index("core").astype(jnp.int32)
+    edges, core, partner = lax.optimization_barrier((edges, core, 1 - core))
+    edges = exchange(edges.reshape(2 * split, columns, width), (*owners, "core"))
+    edges = edges.reshape(split, 2, columns, width)
+    own, right = (
+        lax.dynamic_index_in_dim(edges, at, 1, keepdims=False, allow_negative_indices=False)
+        for at in (partner, core)
+    )
     other = lax.ppermute(own, "core", [(0, 1), (1, 0)])
     stacked = (row_count, per_row * columns, width)
     own, other, right = (a.reshape(stacked) for a in (own, other, right))
@@ -341,7 +347,7 @@
         flops,
         done, own, other, rights,
     )
-    sums = exchange(sums.reshape(split, columns, width))
+    sums = exchange(sums.reshape(split, columns, width), owners)
     return call(
         functools.partial(output_kernel, split, slabs),
         "output",

time: 45.5 us -> 45 us (0.989)
  blocking collectives: 39.4 us -> 38.9 us
    all_to_all x2, blocking collectives: 39.4 us -> 38.9 us  [the longest x1 23.9 us: fast_device(): exchange(edges.reshape(2 * split, columns, width), (*owners, 'core'))]
where the time goes in v5:
time: 45 us; the launch traced here: 44.8 us
  blocking collectives  38.9 us (86%)
  Pallas kernels  4.68 us (10%)
  waiting for transfers between devices  1.01 us (2%)
    all_to_all x1, blocking collectives, fast_device(): exchange(edges.reshape(2 * split, columns, width), (*owners, 'core'))  23.9 us
    all_to_all x1, blocking collectives, fast_device(): sums = exchange(sums.reshape(split, columns, width), owners)  15 us
    pallas_call x4, Pallas kernels, call(): pl.pallas_call(kernel, name=name, out_shape=out_shape, in_specs=specs, ou...  4.68 us
    ppermute x1, waiting for transfers between devices, fast_device(): other = lax.ppermute(own, 'core', [(0, 1), (1, 0)])  1.01 us
  transfers between devices with their start and end apart: 1, of which 1 were waited for; matrix products, arithmetic and copies ran while one was open for 0% of the time, Pallas kernels for 1%

profile of v5, /device:TPU:0, one launch (start us, length us, event | category | flops | bytes accessed | tf_op | source)
XLA Modules:
  0.0 44.8 jit_solution(7146009082837220811)
XLA Ops:
  0.0 2.0 %edges.1 = (bf16[16,2,24,384]{3,2,1,0:T(8,128)(2,1)S(1)}, bf16[48,24,128]{2,1,0:T(8,128)(2,1)S(1)}, bf16[128,128]{1,0:T(8,128)(2,1)S(1)}, f32[1,128]{1,0:T(1,128...) custom-call(bf16[48,24,128]{2,1,0:T(8,128)(2,1)} %x_hbm.1, f32[1,128]{1,0:T(1,128)} %bitcast.19, ...), custom_call_target="tpu_custom_call" | custom-call | flops 150994944 | bytes 1444864 | tf_op jit(solution)/shard_map/edges/pallas_call | solution.py:267
  2.0 23.9 %all_to_all.10 = bf16[32,24,384]{2,1,0:T(8,128)(2,1)S(1)} all-to-all(bf16[32,24,384]{2,1,0:T(8,128)(2,1)S(1)} %bitcast.16), channel_id=1, replica_groups=mesh['row'=4,'col'=2,'depth'=2,'core'=2] {'row','col','depth','core'}, dimensions={0} | all-to-all | bytes 1179648 | tf_op jit(solution)/shard_map/all_to_all | solution.py:321
  25.9 0.1 constant_dynamic-slice_fusion
  26.0 0.1 collective-permute-start
  26.1 0.5 %own.1 = (bf16[4,1,96,128]{3,2,1,0:T(8,128)(2,1)S(1)}, f32[48,24,128]{2,1,0:T(8,128)S(1)}, bf16[2,96,768]{2,1,0:T(8,128)(2,1)S(1)}) custom-call(bf16[4,96,384]{2,1,0:T(8,128)(2,1)S(1)} %bitcast.12, bf16[4,96,384]{2,1,0:T(8,128)(2,1)S(1)} %bitcast.15, bf16[48,24,128]{2,1,0:T(8,128)(2,1)S(1)} %get-tuple-element.21.normed_ref, ...), custom_call_target="tpu_custom_call" | custom-call | flops 75497472 | bytes 1900544 | tf_op jit(solution)/shard_map/own/pallas_call | solution.py:267
  26.6 1.0 %collective-permute-done = bf16[16,24,384]{2,1,0:T(8,128)(2,1)S(1)} collective-permute-done((bf16[16,24,384]{2,1,0:T(8,128)(2,1)S(1)}, bf16[16,24,384]{2,1,0:T(8,128)(2,1)S(1)}, u32[]{:S(2)}, u32[]{:S(2)}) %collective-permute-start) | collective-permute-done | bytes 294944 | tf_op jit(solution)/shard_map/ppermute | solution.py:327
  27.6 0.8 %other.1 = bf16[4,96,384]{2,1,0:T(8,128)(2,1)S(1)} custom-call(bf16[4,1,96,128]{3,2,1,0:T(8,128)(2,1)S(1)} %get-tuple-element.23.done_ref, bf16[4,96,384]{2,1,0:T(8,128)(2,1)S(1)} %bitcast.13, bf16[4,96,384]{2,1,0:T(8,128)(2,1)S(1)} %bitcast.17, bf16[2,96,768]{2,1,0:T(8,128)(2,1)S(1)} %get-tuple-element.24.rights_ref), custom_call_target="tpu_custom_call" | custom-call | flops 75497472 | bytes 1277952 | tf_op jit(solution)/shard_map/other/pallas_call | solution.py:267
  28.4 15.0 %all_to_all.11.sums_ref = bf16[16,24,384]{2,1,0:T(8,128)(2,1)S(1)} all-to-all(bf16[16,24,384]{2,1,0:T(8,128)(2,1)S(1)} %bitcast.14), channel_id=1, replica_groups=mesh['row'=4,'col'=2,'depth'=2,'core'=2] {'row','col','depth'}, dimensions={0} | all-to-all | bytes 589824 | tf_op jit(solution)/shard_map/all_to_all | solution.py:350
  43.4 1.4 %output.1 = bf16[48,24,128]{2,1,0:T(8,128)(2,1)} custom-call(bf16[16,24,384]{2,1,0:T(8,128)(2,1)S(1)} %all_to_all.11.sums_ref, f32[48,24,128]{2,1,0:T(8,128)S(1)} %get-tuple-element.25.gate_ref, f32[1,128]{1,0:T(1,128)S(1)} %get-tuple-element.26.gain_ref, f32[1,128]{1,0:T(1,128)S(1)} %get-tuple-element.27.shift_ref, bf16[128,128]{1,0:T(8,128)(2,1)S(1)} %get-tuple-element.28.w_ref), custom_call_target="tpu_custom_call" | custom-call | flops 37748736 | bytes 1213440 | tf_op jit(solution)/shard_map/output/pallas_call | solution.py:267
Async XLA Ops:
  26.0 1.6 %collective-permute-start = (bf16[16,24,384]{2,1,0:T(8,128)(2,1)S(1)}, bf16[16,24,384]{2,1,0:T(8,128)(2,1)S(1)}, u32[]{:S(2)}, u32[]{:S(2)}) collective-permute-start(bf16[16,24,384]{2,1,0:T(8,128)(2,1)S(1)} %bitcast.11), channel_id=1, source_target_pairs={{0,1},{1,0},{2,3},{3,2},{4,5},{5,4},{6,7},{7,6},{8,9},{9,8},{10,11... | collective-permute-start | bytes 884744 | tf_op jit(solution)/shard_map/ppermute | solution.py:327

commit v6 on v5

--- a/solution.py
+++ b/solution.py
@@ -113,8 +113,10 @@
             for s, tile in enumerate(spread(tiles)):
                 at = slice(i_tile * ROWS, (i_tile + 1) * ROWS)
                 lanes = slice(slab * LANES, (slab + 1) * LANES)
-                out_ref[s, 1 - core, at, lanes] = tile[:ROWS]
-                out_ref[s, core, at, lanes] = tile[ROWS:]
+                depth_count, _, col_count, row_count = out_ref.shape[:4]
+                depth, col, row = s % depth_count, s // depth_count % col_count, s // depth_count // col_count
+                out_ref[depth, 1 - core, col, row, at, lanes] = tile[:ROWS]
+                out_ref[depth, core, col, row, at, lanes] = tile[ROWS:]
     for copy in copies[4:]:
         copy.wait()
 
@@ -280,7 +282,8 @@
     rows, columns, channels = pair_input.shape
     row_count = lax.axis_size("row")
     owners = ("row", "col", "depth")
-    split = row_count * lax.axis_size("col") * lax.axis_size("depth")
+    col_count, depth_count = lax.axis_size("col"), lax.axis_size("depth")
+    split = row_count * col_count * depth_count
     width = rows // split * LANES
     per_row = split // row_count
     slabs = pieces_of(split, columns, rows // (2 * columns))
@@ -294,7 +297,7 @@
         functools.partial(edges_kernel, split),
         "edges",
         (
-            shape((split, 2, columns, width), bf16),
+            shape((depth_count, 2, col_count, row_count, columns, width), bf16),
             shape(pair_input.shape, bf16),
             shape(w_gate.shape, bf16),
             shape((1, channels), f32),
@@ -318,10 +321,14 @@
     exchange = functools.partial(lax.all_to_all, split_axis=0, concat_axis=0, tiled=True)
     core = lax.axis_index("core").astype(jnp.int32)
     edges, core, partner = lax.optimization_barrier((edges, core, 1 - core))
-    edges = exchange(edges.reshape(2 * split, columns, width), (*owners, "core"))
-    edges = edges.reshape(split, 2, columns, width)
+    grouped = edges.shape
+    edges = exchange(
+        edges.reshape(2 * split, columns, width), ("depth", "core", "col", "row")
+    ).reshape(grouped)
     own, right = (
         lax.dynamic_index_in_dim(edges, at, 1, keepdims=False, allow_negative_indices=False)
+        .transpose(2, 1, 0, 3, 4)
+        .reshape(split, columns, width)
         for at in (partner, core)
     )
     other = lax.ppermute(own, "core", [(0, 1), (1, 0)])

time: 45 us -> 44.5 us (0.989)
  blocking collectives: 38.9 us -> 38.4 us
    all_to_all x1, blocking collectives: 15 us -> 14.2 us  [fast_device(): sums = exchange(sums.reshape(split, columns, width), owners)]
where the time goes in v6:
time: 44.5 us; the launch traced here: 44.3 us
  blocking collectives  38.4 us (86%)
  Pallas kernels  4.65 us (10%)
  waiting for transfers between devices  0.66 us (1%)
    all_to_all x1, blocking collectives, fast_device(): exchange(edges.reshape(2 * split, columns, width), ('depth', 'core', 'col...  24.2 us
    all_to_all x1, blocking collectives, fast_device(): sums = exchange(sums.reshape(split, columns, width), owners)  14.2 us
    pallas_call x4, Pallas kernels, call(): pl.pallas_call(kernel, name=name, out_shape=out_shape, in_specs=specs, ou...  4.65 us
  transfers between devices with their start and end apart: 1, of which 1 were waited for; matrix products, arithmetic and copies ran while one was open for 0% of the time, Pallas kernels for 1%

profile of v6, /device:TPU:0, one launch (start us, length us, event | category | flops | bytes accessed | tf_op | source)
XLA Modules:
  0.0 44.3 jit_solution(12359387951802400036)
XLA Ops:
  0.0 1.9 %edges.1 = (bf16[2,2,2,4,24,384]{5,4,3,2,1,0:T(8,128)(2,1)S(1)}, bf16[48,24,128]{2,1,0:T(8,128)(2,1)S(1)}, bf16[128,128]{1,0:T(8,128)(2,1)S(1)}, f32[1,128]{1,0:...) custom-call(bf16[48,24,128]{2,1,0:T(8,128)(2,1)} %x_hbm.1, f32[1,128]{1,0:T(1,128)} %bitcast.28, ...), custom_call_target="tpu_custom_call" | custom-call | flops 150994944 | bytes 1444864 | tf_op jit(solution)/shard_map/edges/pallas_call | solution.py:269
  1.9 24.2 %all_to_all.10 = bf16[32,24,384]{2,1,0:T(8,128)(2,1)S(1)} all-to-all(bf16[32,24,384]{2,1,0:T(8,128)(2,1)S(1)} %bitcast.25), channel_id=1, replica_groups=mesh['row'=4,'col'=2,'depth'=2,'core'=2] {'depth','core','col','row'}, dimensions={0} | all-to-all | bytes 1179648 | tf_op jit(solution)/shard_map/all_to_all | solution.py:325
  26.1 0.1 constant_dynamic-slice_fusion
  26.2 0.4 collective-permute-start
  26.7 0.5 %own.1 = (bf16[4,1,96,128]{3,2,1,0:T(8,128)(2,1)S(1)}, f32[48,24,128]{2,1,0:T(8,128)S(1)}, bf16[2,96,768]{2,1,0:T(8,128)(2,1)S(1)}) custom-call(bf16[4,96,384]{2,1,0:T(8,128)(2,1)S(1)} %bitcast.21, bf16[4,96,384]{2,1,0:T(8,128)(2,1)S(1)} %bitcast.23, bf16[48,24,128]{2,1,0:T(8,128)(2,1)S(1)} %get-tuple-element.21.normed_ref, ...), custom_call_target="tpu_custom_call" | custom-call | flops 75497472 | bytes 1900544 | tf_op jit(solution)/shard_map/own/pallas_call | solution.py:269
  27.2 0.7 %collective-permute-done = bf16[16,24,384]{2,1,0:T(8,128)(2,1)S(1)} collective-permute-done((bf16[16,24,384]{2,1,0:T(8,128)(2,1)S(1)}, bf16[16,24,384]{2,1,0:T(8,128)(2,1)S(1)}, u32[]{:S(2)}, u32[]{:S(2)}) %collective-permute-start) | collective-permute-done | bytes 294944 | tf_op jit(solution)/shard_map/ppermute | solution.py:334
  27.9 0.8 %other.1 = bf16[4,96,384]{2,1,0:T(8,128)(2,1)S(1)} custom-call(bf16[4,1,96,128]{3,2,1,0:T(8,128)(2,1)S(1)} %get-tuple-element.23.done_ref, bf16[4,96,384]{2,1,0:T(8,128)(2,1)S(1)} %bitcast.22, bf16[4,96,384]{2,1,0:T(8,128)(2,1)S(1)} %bitcast.26, bf16[2,96,768]{2,1,0:T(8,128)(2,1)S(1)} %get-tuple-element.24.rights_ref), custom_call_target="tpu_custom_call" | custom-call | flops 75497472 | bytes 1277952 | tf_op jit(solution)/shard_map/other/pallas_call | solution.py:269
  28.7 14.2 %all_to_all.11.sums_ref = bf16[16,24,384]{2,1,0:T(8,128)(2,1)S(1)} all-to-all(bf16[16,24,384]{2,1,0:T(8,128)(2,1)S(1)} %bitcast.24), channel_id=1, replica_groups=mesh['row'=4,'col'=2,'depth'=2,'core'=2] {'row','col','depth'}, dimensions={0} | all-to-all | bytes 589824 | tf_op jit(solution)/shard_map/all_to_all | solution.py:357
  42.9 1.4 %output.1 = bf16[48,24,128]{2,1,0:T(8,128)(2,1)} custom-call(bf16[16,24,384]{2,1,0:T(8,128)(2,1)S(1)} %all_to_all.11.sums_ref, f32[48,24,128]{2,1,0:T(8,128)S(1)} %get-tuple-element.25.gate_ref, f32[1,128]{1,0:T(1,128)S(1)} %get-tuple-element.26.gain_ref, f32[1,128]{1,0:T(1,128)S(1)} %get-tuple-element.27.shift_ref, bf16[128,128]{1,0:T(8,128)(2,1)S(1)} %get-tuple-element.28.w_ref), custom_call_target="tpu_custom_call" | custom-call | flops 37748736 | bytes 1213440 | tf_op jit(solution)/shard_map/output/pallas_call | solution.py:269
  (2 shorter events, 0.1 us)
Async XLA Ops:
  26.2 1.6 %collective-permute-start = (bf16[16,24,384]{2,1,0:T(8,128)(2,1)S(1)}, bf16[16,24,384]{2,1,0:T(8,128)(2,1)S(1)}, u32[]{:S(2)}, u32[]{:S(2)}) collective-permute-start(bf16[16,24,384]{2,1,0:T(8,128)(2,1)S(1)} %bitcast.20), channel_id=1, source_target_pairs={{0,1},{1,0},{2,3},{3,2},{4,5},{5,4},{6,7},{7,6},{8,9},{9,8},{10,11... | collective-permute-start | bytes 884744 | tf_op jit(solution)/shard_map/ppermute | solution.py:334

commit v7 on v6

--- a/solution.py
+++ b/solution.py
@@ -11,6 +11,9 @@
 LANES = 128
 ROWS = 8
 VMEM_LIMIT = 24 * 1024 * 1024
+OWNERS = ("row_hi", "row_lo", "col", "depth")
+FIRST_ORDER = ("depth", "core", "col", "row_hi", "row_lo")
+LAST_ORDER = ("depth", "col", "row_lo", "row_hi")
 NT = (((1,), (1,)), ((), ()))
 
 
@@ -189,7 +192,7 @@
 def own_kernel(split, own_ref, right_ref, normed_ref, wg_ref, out_ref, gate_ref, rights_ref):
     row_count, rows, _ = own_ref.shape
     columns = rows // row_count
-    place = place_in("row", "col", "depth")
+    place = place_in(*OWNERS)
     rights = fold(k_tiles(right_ref, slice(None)), place)
     for half in range(2):
         rights_ref[half] = rights[half]
@@ -209,7 +212,7 @@
 def other_kernel(split, slabs, done_ref, own_ref, other_ref, rights_ref, out_ref):
     row_count, rows, _ = own_ref.shape
     columns = rows // row_count
-    place = place_in("row", "col", "depth")
+    place = place_in(*OWNERS)
     rights = [rights_ref[half] for half in range(2)]
     refs = (own_ref, other_ref)
     done = done_ref.shape[1]
@@ -230,7 +233,7 @@
 
 
 def output_kernel(split, slabs, sums_ref, gate_ref, gain_ref, shift_ref, w_ref, out_ref):
-    columns = sums_ref.shape[1]
+    depth_count, col_count, low_count, _, columns, _ = sums_ref.shape
     channels = out_ref.shape[2]
     parity = 1 - lax.axis_index("core")
 
@@ -252,7 +255,12 @@
         both = units[start : start + 2]
         tiles = []
         for s in range(split):
-            parts = [sums_ref[s, js, n * LANES : (n + 1) * LANES] for n, js in both]
+            rest, depth = divmod(s, depth_count)
+            rest, col = divmod(rest, col_count)
+            high, low = divmod(rest, low_count)
+            parts = [
+                sums_ref[depth, col, low, high, js, n * LANES : (n + 1) * LANES] for n, js in both
+            ]
             tiles.append(turn(jnp.concatenate(parts, axis=0), s))
         tiles = [turn(tile, -i) for i, tile in enumerate(spread(tiles))]
         for at, (n, js) in enumerate(both):
@@ -280,9 +288,8 @@
 
 def fast_device(pair_input, in_gain, in_shift, w_proj, w_gate, out_gain, out_shift, w_out):
     rows, columns, channels = pair_input.shape
-    row_count = lax.axis_size("row")
-    owners = ("row", "col", "depth")
-    col_count, depth_count = lax.axis_size("col"), lax.axis_size("depth")
+    high_count, low_count, col_count, depth_count = (lax.axis_size(axis) for axis in OWNERS)
+    row_count = high_count * low_count
     split = row_count * col_count * depth_count
     width = rows // split * LANES
     per_row = split // row_count
@@ -323,7 +330,7 @@
     edges, core, partner = lax.optimization_barrier((edges, core, 1 - core))
     grouped = edges.shape
     edges = exchange(
-        edges.reshape(2 * split, columns, width), ("depth", "core", "col", "row")
+        edges.reshape(2 * split, columns, width), FIRST_ORDER
     ).reshape(grouped)
     own, right = (
         lax.dynamic_index_in_dim(edges, at, 1, keepdims=False, allow_negative_indices=False)
@@ -354,7 +361,10 @@
         flops,
         done, own, other, rights,
     )
-    sums = exchange(sums.reshape(split, columns, width), owners)
+    sums = sums.reshape(high_count, low_count, col_count, depth_count, columns, width)
+    sums = sums.transpose(3, 2, 1, 0, 4, 5)
+    grouped = sums.shape
+    sums = exchange(sums.reshape(split, columns, width), LAST_ORDER).reshape(grouped)
     return call(
         functools.partial(output_kernel, split, slabs),
         "output",
@@ -389,10 +399,11 @@
         if suits(mesh, pair_input, w_proj):
             row_count, col_count, depth_count = mesh.devices.shape
             used = Mesh(
-                mesh.devices.reshape(row_count, col_count, depth_count // 2, 2),
-                ("row", "col", "depth", "core"),
+                mesh.devices.reshape(row_count // 2, 2, col_count, depth_count // 2, 2),
+                (*OWNERS, "core"),
             )
-            pair, body = P("row", ("col", "depth", "core"), None), fast_device
+            pair = P(("row_hi", "row_lo"), ("col", "depth", "core"), None)
+            body = fast_device
         else:
             used, pair, body = mesh, P("row", ("col", "depth"), None), plain_device
         return jax.shard_map(

time: 44.5 us -> 43.8 us (0.984)
  blocking collectives: 38.4 us -> 37.7 us
    all_to_all x2, blocking collectives: 38.4 us -> 37.7 us  [the longest x1 24.2 us: fast_device(): exchange(edges.reshape(2 * split, columns, width), FIRST_ORDER)]
where the time goes in v7:
time: 43.8 us; the launch traced here: 43.6 us
  blocking collectives  37.7 us (86%)
  Pallas kernels  4.65 us (11%)
  waiting for transfers between devices  0.66 us (2%)
    all_to_all x1, blocking collectives, fast_device(): exchange(edges.reshape(2 * split, columns, width), FIRST_ORDER)  24.2 us
    all_to_all x1, blocking collectives, fast_device(): exchange(sums.reshape(split, columns, width), LAST_ORDER).reshape(grouped)  13.5 us
    pallas_call x4, Pallas kernels, call(): pl.pallas_call(kernel, name=name, out_shape=out_shape, in_specs=specs, ou...  4.65 us
  transfers between devices with their start and end apart: 1, of which 1 were waited for; matrix products, arithmetic and copies ran while one was open for 0% of the time, Pallas kernels for 1%

profile of v7, /device:TPU:0, one launch (start us, length us, event | category | flops | bytes accessed | tf_op | source)
XLA Modules:
  0.0 43.6 jit_solution(5607809226237841538)
XLA Ops:
  0.0 1.9 %edges.1 = (bf16[2,2,2,4,24,384]{5,4,3,2,1,0:T(8,128)(2,1)S(1)}, bf16[48,24,128]{2,1,0:T(8,128)(2,1)S(1)}, bf16[128,128]{1,0:T(8,128)(2,1)S(1)}, f32[1,128]{1,0:...) custom-call(bf16[48,24,128]{2,1,0:T(8,128)(2,1)} %x_hbm.1, f32[1,128]{1,0:T(1,128)} %bitcast.34, ...), custom_call_target="tpu_custom_call" | custom-call | flops 150994944 | bytes 1444864 | tf_op jit(solution)/shard_map/edges/pallas_call | solution.py:277
  1.9 24.2 %all_to_all.10 = bf16[32,24,384]{2,1,0:T(8,128)(2,1)S(1)} all-to-all(bf16[32,24,384]{2,1,0:T(8,128)(2,1)S(1)} %bitcast.30), channel_id=1, replica_groups=mesh['row_hi'=2,'row_lo'=2,'col'=2,'depth'=2,'core'=2] {'depth','core','..., dimensions={0} | all-to-all | bytes 1179648 | tf_op jit(solution)/shard_map/all_to_all | solution.py:332
  26.1 0.1 constant_dynamic-slice_fusion
  26.2 0.4 collective-permute-start
  26.7 0.5 %own.1 = (bf16[4,1,96,128]{3,2,1,0:T(8,128)(2,1)S(1)}, f32[48,24,128]{2,1,0:T(8,128)S(1)}, bf16[2,96,768]{2,1,0:T(8,128)(2,1)S(1)}) custom-call(bf16[4,96,384]{2,1,0:T(8,128)(2,1)S(1)} %bitcast.25, bf16[4,96,384]{2,1,0:T(8,128)(2,1)S(1)} %bitcast.27, bf16[48,24,128]{2,1,0:T(8,128)(2,1)S(1)} %get-tuple-element.21.normed_ref, ...), custom_call_target="tpu_custom_call" | custom-call | flops 75497472 | bytes 1900544 | tf_op jit(solution)/shard_map/own/pallas_call | solution.py:277
  27.2 0.7 %collective-permute-done = bf16[16,24,384]{2,1,0:T(8,128)(2,1)S(1)} collective-permute-done((bf16[16,24,384]{2,1,0:T(8,128)(2,1)S(1)}, bf16[16,24,384]{2,1,0:T(8,128)(2,1)S(1)}, u32[]{:S(2)}, u32[]{:S(2)}) %collective-permute-start) | collective-permute-done | bytes 294944 | tf_op jit(solution)/shard_map/ppermute | solution.py:341
  27.9 0.8 %other.1 = bf16[4,96,384]{2,1,0:T(8,128)(2,1)S(1)} custom-call(bf16[4,1,96,128]{3,2,1,0:T(8,128)(2,1)S(1)} %get-tuple-element.23.done_ref, bf16[4,96,384]{2,1,0:T(8,128)(2,1)S(1)} %bitcast.26, bf16[4,96,384]{2,1,0:T(8,128)(2,1)S(1)} %bitcast.31, bf16[2,96,768]{2,1,0:T(8,128)(2,1)S(1)} %get-tuple-element.24.rights_ref), custom_call_target="tpu_custom_call" | custom-call | flops 75497472 | bytes 1277952 | tf_op jit(solution)/shard_map/other/pallas_call | solution.py:277
  28.7 13.5 %all_to_all.11 = bf16[16,24,384]{2,1,0:T(8,128)(2,1)S(1)} all-to-all(bf16[16,24,384]{2,1,0:T(8,128)(2,1)S(1)} %bitcast.33), channel_id=1, replica_groups=mesh['row_hi'=2,'row_lo'=2,'col'=2,'depth'=2,'core'=2] {'depth','col','r..., dimensions={0} | all-to-all | bytes 589824 | tf_op jit(solution)/shard_map/all_to_all | solution.py:367
  42.2 1.4 %output.1 = bf16[48,24,128]{2,1,0:T(8,128)(2,1)} custom-call(bf16[2,2,2,2,24,384]{5,4,3,2,1,0:T(8,128)(2,1)S(1)} %bitcast.29, f32[48,24,128]{2,1,0:T(8,128)S(1)} %get-tuple-element.25.gate_ref, f32[1,128]{1,0:T(1,128)S(1)} %get-tuple-element.26.gain_ref, f32[1,128]{1,0:T(1,128)S(1)} %get-tuple-element.27.shift_ref, bf16[128,128]{1,0:T(8,128)(2,1)S(1)} %get-tuple-element.28.w_ref), custom_call_target="tpu_custom_call" | custom-call | flops 37748736 | bytes 1213440 | tf_op jit(solution)/shard_map/output/pallas_call | solution.py:277
  (3 shorter events, 0.1 us)
Async XLA Ops:
  26.2 1.6 %collective-permute-start = (bf16[16,24,384]{2,1,0:T(8,128)(2,1)S(1)}, bf16[16,24,384]{2,1,0:T(8,128)(2,1)S(1)}, u32[]{:S(2)}, u32[]{:S(2)}) collective-permute-start(bf16[16,24,384]{2,1,0:T(8,128)(2,1)S(1)} %bitcast.24), channel_id=1, source_target_pairs={{0,1},{1,0},{2,3},{3,2},{4,5},{5,4},{6,7},{7,6},{8,9},{9,8},{10,11... | collective-permute-start | bytes 884744 | tf_op jit(solution)/shard_map/ppermute | solution.py:341

commit v8 on v7

--- a/solution.py
+++ b/solution.py
@@ -332,12 +332,12 @@
     edges = exchange(
         edges.reshape(2 * split, columns, width), FIRST_ORDER
     ).reshape(grouped)
-    own, right = (
-        lax.dynamic_index_in_dim(edges, at, 1, keepdims=False, allow_negative_indices=False)
-        .transpose(2, 1, 0, 3, 4)
-        .reshape(split, columns, width)
-        for at in (partner, core)
-    )
+    def side(array, at):
+        piece = lax.dynamic_index_in_dim(array, at, 1, keepdims=False, allow_negative_indices=False)
+        return piece.transpose(2, 1, 0, 3, 4).reshape(split, columns, width)
+
+    own, edges = lax.optimization_barrier((side(edges, partner), edges))
+    right = side(edges, core)
     other = lax.ppermute(own, "core", [(0, 1), (1, 0)])
     stacked = (row_count, per_row * columns, width)
     own, other, right = (a.reshape(stacked) for a in (own, other, right))

time: 43.8 us -> 43.8 us (level)
  no operation moved by 1% of the time
where the time goes in v8:
time: 43.8 us; the launch traced here: 43.6 us
  blocking collectives  37.7 us (86%)
  Pallas kernels  4.65 us (11%)
  waiting for transfers between devices  0.66 us (2%)
    all_to_all x1, blocking collectives, fast_device(): exchange(edges.reshape(2 * split, columns, width), FIRST_ORDER)  24.2 us
    all_to_all x1, blocking collectives, fast_device(): exchange(sums.reshape(split, columns, width), LAST_ORDER).reshape(grouped)  13.5 us
    pallas_call x4, Pallas kernels, call(): pl.pallas_call(kernel, name=name, out_shape=out_shape, in_specs=specs, ou...  4.65 us
  transfers between devices with their start and end apart: 1, of which 1 were waited for; matrix products, arithmetic and copies ran while one was open for 0% of the time, Pallas kernels for 1%

profile of v8, /device:TPU:0, one launch (start us, length us, event | category | flops | bytes accessed | tf_op | source)
XLA Modules:
  0.0 43.6 jit_solution(11825580139952981413)
XLA Ops:
  0.0 1.9 %edges.1 = (bf16[2,2,2,4,24,384]{5,4,3,2,1,0:T(8,128)(2,1)S(1)}, bf16[48,24,128]{2,1,0:T(8,128)(2,1)S(1)}, bf16[128,128]{1,0:T(8,128)(2,1)S(1)}, f32[1,128]{1,0:...) custom-call(bf16[48,24,128]{2,1,0:T(8,128)(2,1)} %x_hbm.1, f32[1,128]{1,0:T(1,128)} %bitcast.34, ...), custom_call_target="tpu_custom_call" | custom-call | flops 150994944 | bytes 1444864 | tf_op jit(solution)/shard_map/edges/pallas_call | solution.py:277
  1.9 24.2 %all_to_all.10 = bf16[32,24,384]{2,1,0:T(8,128)(2,1)S(1)} all-to-all(bf16[32,24,384]{2,1,0:T(8,128)(2,1)S(1)} %bitcast.29), channel_id=1, replica_groups=mesh['row_hi'=2,'row_lo'=2,'col'=2,'depth'=2,'core'=2] {'depth','core','..., dimensions={0} | all-to-all | bytes 1179648 | tf_op jit(solution)/shard_map/all_to_all | solution.py:332
  26.2 0.4 collective-permute-start
  26.6 0.5 %own.1 = (bf16[4,1,96,128]{3,2,1,0:T(8,128)(2,1)S(1)}, f32[48,24,128]{2,1,0:T(8,128)S(1)}, bf16[2,96,768]{2,1,0:T(8,128)(2,1)S(1)}) custom-call(bf16[4,96,384]{2,1,0:T(8,128)(2,1)S(1)} %bitcast.24, bf16[4,96,384]{2,1,0:T(8,128)(2,1)S(1)} %bitcast.26, bf16[48,24,128]{2,1,0:T(8,128)(2,1)S(1)} %get-tuple-element.25.normed_ref, ...), custom_call_target="tpu_custom_call" | custom-call | flops 75497472 | bytes 1900544 | tf_op jit(solution)/shard_map/own/pallas_call | solution.py:277
  27.2 0.7 %collective-permute-done = bf16[16,24,384]{2,1,0:T(8,128)(2,1)S(1)} collective-permute-done((bf16[16,24,384]{2,1,0:T(8,128)(2,1)S(1)}, bf16[16,24,384]{2,1,0:T(8,128)(2,1)S(1)}, u32[]{:S(2)}, u32[]{:S(2)}) %collective-permute-start) | collective-permute-done | bytes 294944 | tf_op jit(solution)/shard_map/ppermute | solution.py:341
  27.9 0.8 %other.1 = bf16[4,96,384]{2,1,0:T(8,128)(2,1)S(1)} custom-call(bf16[4,1,96,128]{3,2,1,0:T(8,128)(2,1)S(1)} %get-tuple-element.27.done_ref, bf16[4,96,384]{2,1,0:T(8,128)(2,1)S(1)} %bitcast.25, bf16[4,96,384]{2,1,0:T(8,128)(2,1)S(1)} %bitcast.30, bf16[2,96,768]{2,1,0:T(8,128)(2,1)S(1)} %get-tuple-element.28.rights_ref), custom_call_target="tpu_custom_call" | custom-call | flops 75497472 | bytes 1277952 | tf_op jit(solution)/shard_map/other/pallas_call | solution.py:277
  28.7 13.5 %all_to_all.11 = bf16[16,24,384]{2,1,0:T(8,128)(2,1)S(1)} all-to-all(bf16[16,24,384]{2,1,0:T(8,128)(2,1)S(1)} %bitcast.33), channel_id=1, replica_groups=mesh['row_hi'=2,'row_lo'=2,'col'=2,'depth'=2,'core'=2] {'depth','col','r..., dimensions={0} | all-to-all | bytes 589824 | tf_op jit(solution)/shard_map/all_to_all | solution.py:367
  42.2 1.4 %output.1 = bf16[48,24,128]{2,1,0:T(8,128)(2,1)} custom-call(bf16[2,2,2,2,24,384]{5,4,3,2,1,0:T(8,128)(2,1)S(1)} %bitcast.28, f32[48,24,128]{2,1,0:T(8,128)S(1)} %get-tuple-element.29.gate_ref, f32[1,128]{1,0:T(1,128)S(1)} %get-tuple-element.30.gain_ref, f32[1,128]{1,0:T(1,128)S(1)} %get-tuple-element.31.shift_ref, bf16[128,128]{1,0:T(8,128)(2,1)S(1)} %get-tuple-element.32.w_ref), custom_call_target="tpu_custom_call" | custom-call | flops 37748736 | bytes 1213440 | tf_op jit(solution)/shard_map/output/pallas_call | solution.py:277
  (4 shorter events, 0.1 us)
Async XLA Ops:
  26.2 1.6 %collective-permute-start = (bf16[16,24,384]{2,1,0:T(8,128)(2,1)S(1)}, bf16[16,24,384]{2,1,0:T(8,128)(2,1)S(1)}, u32[]{:S(2)}, u32[]{:S(2)}) collective-permute-start(bf16[16,24,384]{2,1,0:T(8,128)(2,1)S(1)} %bitcast.23), channel_id=1, source_target_pairs={{0,1},{1,0},{2,3},{3,2},{4,5},{5,4},{6,7},{7,6},{8,9},{9,8},{10,11... | collective-permute-start | bytes 884744 | tf_op jit(solution)/shard_map/ppermute | solution.py:341

commit v9 on v8

--- a/solution.py
+++ b/solution.py
@@ -189,47 +189,65 @@
     return [order[n : n + per] for n in range(0, len(order), per)]
 
 
+def column_units(ref, split):
+    row_count, rows, _ = ref.shape
+    columns = rows // row_count
+    whole = columns // split * split
+    units = [
+        k_tiles(ref, slice(target * columns + first, target * columns + first + split))
+        for target in range(row_count)
+        for first in range(0, whole, split)
+    ]
+    for target in range(0, row_count, 2):
+        halves = [
+            k_tiles(ref, slice((target + n) * columns + whole, (target + n + 1) * columns))
+            for n in range(2)
+        ]
+        units.append([jnp.concatenate(parts, axis=0) for parts in zip(*halves)])
+    return units
+
+
 def own_kernel(split, own_ref, right_ref, normed_ref, wg_ref, out_ref, gate_ref, rights_ref):
-    row_count, rows, _ = own_ref.shape
-    columns = rows // row_count
     place = place_in(*OWNERS)
     rights = fold(k_tiles(right_ref, slice(None)), place)
     for half in range(2):
         rights_ref[half] = rights[half]
-    slots = [(target, slab) for target in range(row_count) for slab in range(out_ref.shape[1])]
-    units = []
-    for target, slab in slots:
-        first = target * columns + slab * split
-        units.append(k_tiles(own_ref, slice(first, first + split)))
-    for (target, slab), block in zip(slots, slab_products(split, place, rights, units)):
-        out_ref[target, slab] = block
+    blocks = slab_products(split, place, rights, column_units(own_ref, split))
+    for unit, block in enumerate(blocks):
+        out_ref[unit] = block
     rows, columns, channels = normed_ref.shape
     normed = normed_ref[...].reshape(rows * columns, channels)
     gate = jax.nn.sigmoid(jnp.dot(normed, wg_ref[...], preferred_element_type=jnp.float32))
     gate_ref[...] = gate.reshape(rows, columns, channels)
 
 
-def other_kernel(split, slabs, done_ref, own_ref, other_ref, rights_ref, out_ref):
-    row_count, rows, _ = own_ref.shape
-    columns = rows // row_count
+def other_kernel(split, done_ref, other_ref, rights_ref, out_ref):
+    row_count, rows, _ = other_ref.shape
     place = place_in(*OWNERS)
     rights = [rights_ref[half] for half in range(2)]
-    refs = (own_ref, other_ref)
-    done = done_ref.shape[1]
-    for start in range(0, row_count, 2):
-        slots, units = [], []
-        for target in (start, start + 1):
-            for slab in range(done):
-                out_ref[target, :, slab * LANES : (slab + 1) * LANES] = done_ref[target, slab]
-            for slab in range(done, len(slabs)):
-                pieces = [
-                    k_tiles(refs[core], slice(target * columns + first, target * columns + first + ROWS))
-                    for core, first in slabs[slab]
-                ]
-                slots.append((target, slab))
-                units.append([jnp.concatenate(parts, axis=0) for parts in zip(*pieces)])
-        for (target, slab), block in zip(slots, slab_products(split, place, rights, units)):
-            out_ref[target, :, slab * LANES : (slab + 1) * LANES] = block
+    blocks = slab_products(split, place, rights, column_units(other_ref, split))
+    whole = rows // row_count // split
+    depth_count, col_count, low_count, _, columns, width = out_ref.shape
+    last = width - LANES
+    lower = lax.broadcasted_iota(jnp.int32, (rows, LANES), 1) & (split // 2) == 0
+
+    def store(target, lane, block):
+        high, low = divmod(target, low_count)
+        for cy in range(col_count * depth_count):
+            col, depth = divmod(cy, depth_count)
+            piece = block[cy * columns : (cy + 1) * columns]
+            out_ref[depth, col, low, high, :, lane : lane + LANES] = piece
+
+    for target in range(row_count):
+        for slab in range(whole):
+            unit = target * whole + slab
+            store(target, slab * LANES, done_ref[unit])
+            store(target, (whole + slab) * LANES, blocks[unit])
+    for pair in range(row_count // 2):
+        unit = row_count * whole + pair
+        firsts, seconds = done_ref[unit], blocks[unit]
+        store(2 * pair, last, jnp.where(lower, firsts, turn(seconds, split // 2)))
+        store(2 * pair + 1, last, jnp.where(lower, turn(firsts, -(split // 2)), seconds))
 
 
 def output_kernel(split, slabs, sums_ref, gate_ref, gain_ref, shift_ref, w_ref, out_ref):
@@ -294,7 +312,7 @@
     width = rows // split * LANES
     per_row = split // row_count
     slabs = pieces_of(split, columns, rows // (2 * columns))
-    own_slabs = sum(all(core == 0 for core, _ in slab) for slab in slabs)
+    units = row_count * (rows // 2 // split) + row_count // 2
     bf16, f32 = jnp.bfloat16, jnp.float32
     shape = jax.ShapeDtypeStruct
     gains = [a.reshape(1, channels) for a in (in_gain, in_shift, out_gain, out_shift)]
@@ -345,7 +363,7 @@
         functools.partial(own_kernel, split),
         "own",
         (
-            shape((row_count, own_slabs, per_row * columns, LANES), bf16),
+            shape((units, per_row * columns, LANES), bf16),
             shape(pair_input.shape, f32),
             shape((2, per_row * columns, row_count * width // 2), bf16),
         ),
@@ -354,15 +372,13 @@
         own, right, normed, wg,
     )
     sums = call(
-        functools.partial(other_kernel, split, slabs),
+        functools.partial(other_kernel, split),
         "other",
-        shape(stacked, bf16),
-        [VMEM] * 4,
+        shape((depth_count, col_count, low_count, high_count, columns, width), bf16),
+        [VMEM] * 3,
         flops,
-        done, own, other, rights,
-    )
-    sums = sums.reshape(high_count, low_count, col_count, depth_count, columns, width)
-    sums = sums.transpose(3, 2, 1, 0, 4, 5)
+        done, other, rights,
+    )
     grouped = sums.shape
     sums = exchange(sums.reshape(split, columns, width), LAST_ORDER).reshape(grouped)
     return call(
@@ -391,6 +407,7 @@
         and rows % split == 0
         and columns % ROWS == 0
         and rows % (2 * columns) == 0
+        and rows // 2 % split == split // 2
     )
 
 

time: 43.8 us -> 43.6 us (level)
  no operation moved by 1% of the time
where the time goes in v9:
time: 43.6 us; the launch traced here: 43.5 us
  blocking collectives  37.7 us (86%)
  Pallas kernels  4.66 us (11%)
  waiting for transfers between devices  0.58 us (1%)
    all_to_all x1, blocking collectives, fast_device(): exchange(edges.reshape(2 * split, columns, width), FIRST_ORDER)  24.2 us
    all_to_all x1, blocking collectives, fast_device(): exchange(sums.reshape(split, columns, width), LAST_ORDER).reshape(grouped)  13.5 us
    pallas_call x4, Pallas kernels, call(): pl.pallas_call(kernel, name=name, out_shape=out_shape, in_specs=specs, ou...  4.66 us
  transfers between devices with their start and end apart: 1, of which 1 were waited for; matrix products, arithmetic and copies ran while one was open for 0% of the time, Pallas kernels for 1%

profile of v9, /device:TPU:0, one launch (start us, length us, event | category | flops | bytes accessed | tf_op | source)
XLA Modules:
  0.0 43.5 jit_solution(10344078662024399474)
XLA Ops:
  0.0 1.9 %edges.1 = (bf16[2,2,2,4,24,384]{5,4,3,2,1,0:T(8,128)(2,1)S(1)}, bf16[48,24,128]{2,1,0:T(8,128)(2,1)S(1)}, bf16[128,128]{1,0:T(8,128)(2,1)S(1)}, f32[1,128]{1,0:...) custom-call(bf16[48,24,128]{2,1,0:T(8,128)(2,1)} %x_hbm.1, f32[1,128]{1,0:T(1,128)} %bitcast.29, ...), custom_call_target="tpu_custom_call" | custom-call | flops 150994944 | bytes 1444864 | tf_op jit(solution)/shard_map/edges/pallas_call | solution.py:295
  1.9 24.2 %all_to_all.10 = bf16[32,24,384]{2,1,0:T(8,128)(2,1)S(1)} all-to-all(bf16[32,24,384]{2,1,0:T(8,128)(2,1)S(1)} %bitcast.25), channel_id=1, replica_groups=mesh['row_hi'=2,'row_lo'=2,'col'=2,'depth'=2,'core'=2] {'depth','core','..., dimensions={0} | all-to-all | bytes 1179648 | tf_op jit(solution)/shard_map/all_to_all | solution.py:350
  26.2 0.4 collective-permute-start
  26.6 0.6 %own.1 = (bf16[6,96,128]{2,1,0:T(8,128)(2,1)S(1)}, f32[48,24,128]{2,1,0:T(8,128)S(1)}, bf16[2,96,768]{2,1,0:T(8,128)(2,1)S(1)}) custom-call(bf16[4,96,384]{2,1,0:T(8,128)(2,1)S(1)} %bitcast.21, bf16[4,96,384]{2,1,0:T(8,128)(2,1)S(1)} %bitcast.22, bf16[48,24,128]{2,1,0:T(8,128)(2,1)S(1)} %get-tuple-element.25.normed_ref, ...), custom_call_target="tpu_custom_call" | custom-call | flops 75497472 | bytes 1949696 | tf_op jit(solution)/shard_map/own/pallas_call | solution.py:295
  27.3 0.6 %collective-permute-done = bf16[16,24,384]{2,1,0:T(8,128)(2,1)S(1)} collective-permute-done((bf16[16,24,384]{2,1,0:T(8,128)(2,1)S(1)}, bf16[16,24,384]{2,1,0:T(8,128)(2,1)S(1)}, u32[]{:S(2)}, u32[]{:S(2)}) %collective-permute-start) | collective-permute-done | bytes 294944 | tf_op jit(solution)/shard_map/ppermute | solution.py:359
  27.9 0.7 %other.1 = bf16[2,2,2,2,24,384]{5,4,3,2,1,0:T(8,128)(2,1)S(1)} custom-call(bf16[6,96,128]{2,1,0:T(8,128)(2,1)S(1)} %get-tuple-element.27.done_ref, bf16[4,96,384]{2,1,0:T(8,128)(2,1)S(1)} %bitcast.26, bf16[2,96,768]{2,1,0:T(8,128)(2,1)S(1)} %get-tuple-element.28.rights_ref), custom_call_target="tpu_custom_call" | custom-call | flops 75497472 | bytes 1032192 | tf_op jit(solution)/shard_map/other/pallas_call | solution.py:295
  28.5 13.5 %all_to_all.11 = bf16[16,24,384]{2,1,0:T(8,128)(2,1)S(1)} all-to-all(bf16[16,24,384]{2,1,0:T(8,128)(2,1)S(1)} %bitcast.24), channel_id=1, replica_groups=mesh['row_hi'=2,'row_lo'=2,'col'=2,'depth'=2,'core'=2] {'depth','col','r..., dimensions={0} | all-to-all | bytes 589824 | tf_op jit(solution)/shard_map/all_to_all | solution.py:383
  42.0 1.4 %output.1 = bf16[48,24,128]{2,1,0:T(8,128)(2,1)} custom-call(bf16[2,2,2,2,24,384]{5,4,3,2,1,0:T(8,128)(2,1)S(1)} %bitcast.23, f32[48,24,128]{2,1,0:T(8,128)S(1)} %get-tuple-element.29.gate_ref, f32[1,128]{1,0:T(1,128)S(1)} %get-tuple-element.30.gain_ref, f32[1,128]{1,0:T(1,128)S(1)} %get-tuple-element.31.shift_ref, bf16[128,128]{1,0:T(8,128)(2,1)S(1)} %get-tuple-element.32.w_ref), custom_call_target="tpu_custom_call" | custom-call | flops 37748736 | bytes 1213440 | tf_op jit(solution)/shard_map/output/pallas_call | solution.py:295
  (3 shorter events, 0.1 us)
Async XLA Ops:
  26.2 1.6 %collective-permute-start = (bf16[16,24,384]{2,1,0:T(8,128)(2,1)S(1)}, bf16[16,24,384]{2,1,0:T(8,128)(2,1)S(1)}, u32[]{:S(2)}, u32[]{:S(2)}) collective-permute-start(bf16[16,24,384]{2,1,0:T(8,128)(2,1)S(1)} %bitcast.20), channel_id=1, source_target_pairs={{0,1},{1,0},{2,3},{3,2},{4,5},{5,4},{6,7},{7,6},{8,9},{9,8},{10,11... | collective-permute-start | bytes 884744 | tf_op jit(solution)/shard_map/ppermute | solution.py:359
